TPU v7x, 256 devices: a whole 4x4x8 slice. The times are simulated.
256 devices in a mesh: frame: 16 (over x_hi, z), height: 8 (over x_lo, y), dp: 2 (over core).
Axes of the slice: x: 4 (x_hi: 2, x_lo: 2; x = x_hi * 2 + x_lo), y: 4, z: 8, core: 2. Of those that a mesh axis runs over, the one named last changes fastest.
Arguments:
- clip_latents: bfloat16 [2, 32, 128, 16, 320], P('dp', 'frame', 'height'), may hold values from -6 to 6
- out_grad: bfloat16 [2, 32, 128, 16, 320], P('dp', 'frame', 'height'), may hold values from -6 to 6
- box_mask: int32 [2, 32, 128, 16], P('dp', 'frame', 'height'), may hold values from 0 to 1, as said below
- attn_weights: bfloat16 [1280, 320], replicated, may hold values from -0.3125 to 0.3125
- conv_weights: bfloat16 [2880, 320], replicated, may hold values from -0.109375 to 0.109375
- time_bias: float32 [5, 32, 32], replicated, may hold values from -4 to 250
Outputs:
- grad_input: bfloat16 [2, 32, 128, 16, 320], P('dp', 'frame', 'height')
- grad_attn: float32 [1280, 320], P(('frame', 'height', 'dp'))
- grad_conv: float32 [2880, 320], P(('height', 'dp'))
Inputs may be any that keep to these rules, and one draw needn't show every extreme that they name: Each frame of each clip has one grounding box: box_mask is 1 on a rectangle of 32 to 64 rows and 4 to 8 columns, 0 elsewhere.
All inputs are finite; a program needn't handle non-finite values.
Results may differ from a plain program's by a relative error of at most 0.025.
Values may be sent and summed in bfloat16 or wider, within the bound.
A program may use at most 64 MiB of HBM per device.

v0:
```python
import jax
import jax.numpy as jnp
from jax import lax
from jax.sharding import PartitionSpec as P

ground_bias = 2.0


def side_by_side(arrays, axis, split_dim, concat_dim, along):
    columns = [a.reshape(*a.shape[:along], -1) for a in arrays]
    both = jnp.concatenate(columns, axis=along)
    filled, at, gathered = (
        lax.all_to_all(both, axis, split_axis=split_dim, concat_axis=concat_dim, tiled=True),
        0,
        [],
    )
    for a, column in zip(arrays, columns):
        share = filled[..., at : at + column.shape[along]]
        gathered.append(share.reshape(*share.shape[:along], *a.shape[along:]))
        at += column.shape[along]
    return tuple(gathered)


def padded_2(block, sides, width):
    for axis, dim in sides:
        count = lax.axis_size(axis)
        forward = [(i, i + 1) for i in range(count - 1)]
        backward = [(target, source) for source, target in forward]
        low = lax.ppermute(
            lax.slice_in_dim(block, block.shape[dim] - width, None, axis=dim), axis, forward
        )
        high = lax.ppermute(lax.slice_in_dim(block, 0, width, axis=dim), axis, backward)
        block = jnp.concatenate([low, block, high], axis=dim)
    return block


def copy_for_each(array, axis):
    copies = jnp.broadcast_to(array, (lax.axis_size(axis), *array.shape))
    return lax.all_to_all(copies, axis, split_axis=0, concat_axis=0, tiled=True)


def over_copies(array, axis):
    everything = copy_for_each(array, axis)
    return jnp.sum(everything.astype(jnp.float32), axis=0)


def silu_slope(value):
    sig = jax.nn.sigmoid(value)
    return sig * (1.0 + value * (1.0 - sig))


def project(matrix, weight):
    flat_rows = matrix.reshape(-1, matrix.shape[-1])
    result = jnp.dot(flat_rows, weight, preferred_element_type=jnp.float32)
    return result.reshape(matrix.shape[:-1] + (weight.shape[1],))


def project_back(matrix, weight):
    flat_rows = matrix.reshape(-1, matrix.shape[-1])
    result = lax.dot_general(
        flat_rows, weight, (((1,), (1,)), ((), ())), preferred_element_type=jnp.float32
    )
    return result.reshape(matrix.shape[:-1] + (weight.shape[0],))


def cross(left, right):
    left_rows = left.reshape(-1, left.shape[-1])
    right_rows = right.reshape(-1, right.shape[-1])
    return lax.dot_general(
        left_rows, right_rows, (((0,), (0,)), ((), ())), preferred_element_type=jnp.float32
    )


def body(clip_latents, out_grad, box_mask, attn_weights, conv_weights, time_bias):
    clip_count, frame_count, row_count, col_count, channels = clip_latents.shape
    head_count = time_bias.shape[0]
    all_frames = time_bias.shape[1]
    head_size = channels // head_count
    pixels = row_count * col_count
    scaling = head_size ** (-0.5)
    w_query = attn_weights[:channels]
    w_key = attn_weights[channels : 2 * channels]
    w_value = attn_weights[2 * channels : 3 * channels]
    w_out = attn_weights[3 * channels :]
    flat_x = clip_latents.reshape(clip_count, frame_count, pixels, channels)
    flat_marks = box_mask.reshape(clip_count, frame_count, pixels).astype(jnp.bfloat16)
    latents_t, marks_t = side_by_side((flat_x, flat_marks), "frame", 2, 1, 3)
    query_t = project(latents_t, w_query).astype(jnp.bfloat16)
    key_t = project(latents_t, w_key).astype(jnp.bfloat16)
    value_t = project(latents_t, w_value).astype(jnp.bfloat16)
    column_tokens = query_t.shape[2]
    head_shape = (clip_count, all_frames, column_tokens, head_count, head_size)
    qh = query_t.reshape(head_shape)
    kh = key_t.reshape(head_shape)
    vh = value_t.reshape(head_shape)
    mark_bias = ground_bias * jnp.transpose(marks_t.astype(jnp.float32), (0, 2, 1))
    score_bias = time_bias[None, None] + mark_bias[:, :, None, None, :]
    scores = (
        jnp.einsum("ctnhd,cunhd->cnhtu", qh, kh, preferred_element_type=jnp.float32) * scaling
        + score_bias
    )
    prob_full = jax.nn.softmax(scores, axis=-1)
    prob_half = prob_full.astype(jnp.bfloat16)
    mixed_t = jnp.einsum(
        "cnhtu,cunhd->ctnhd", prob_half, vh, preferred_element_type=jnp.float32
    ).astype(jnp.bfloat16)
    mixed_t = mixed_t.reshape(clip_count, all_frames, column_tokens, channels)
    mixed_rows = lax.all_to_all(mixed_t, "frame", split_axis=1, concat_axis=2, tiled=True)
    residual = (flat_x.astype(jnp.float32) + project(mixed_rows, w_out)).astype(jnp.bfloat16)
    activated = jax.nn.silu(residual.astype(jnp.float32)).astype(jnp.bfloat16)
    out_flat = out_grad.reshape(clip_count, frame_count, pixels, channels)
    stacked = jnp.concatenate([activated, out_flat], axis=-1).reshape(
        clip_count, frame_count, row_count, col_count, 2 * channels
    )
    padded = padded_2(stacked, (("height", 2),), 1)
    padded = jnp.pad(padded, ((0, 0), (0, 0), (0, 0), (1, 1), (0, 0)))
    act_pad = padded[..., :channels]
    grad_pad = padded[..., channels:]
    out_rows = out_grad.reshape(-1, channels)
    delta_sum = jnp.zeros((out_rows.shape[0], channels), jnp.float32)
    conv_terms = []
    for row_step in (-1, 0, 1):
        for col_step in (-1, 0, 1):
            tap_index = 3 * (row_step + 1) + col_step + 1
            tap_weight = conv_weights[tap_index * channels : (tap_index + 1) * channels]
            shifted = grad_pad[
                :,
                :,
                1 - row_step : 1 - row_step + row_count,
                1 - col_step : 1 - col_step + col_count,
                :,
            ]
            delta_sum = delta_sum + project_back(shifted.reshape(-1, channels), tap_weight)
            moved_rows = act_pad[
                :,
                :,
                1 + row_step : 1 + row_step + row_count,
                1 + col_step : 1 + col_step + col_count,
                :,
            ]
            conv_terms.append(cross(moved_rows, out_rows))
    residual_flat = residual.reshape(-1, channels).astype(jnp.float32)
    upstream = (out_rows.astype(jnp.float32) + silu_slope(residual_flat) * delta_sum).astype(
        jnp.bfloat16
    )
    d_mixed = (
        project_back(upstream, w_out)
        .astype(jnp.bfloat16)
        .reshape(clip_count, frame_count, pixels, channels)
    )
    d_mixed_t = lax.all_to_all(d_mixed, "frame", split_axis=2, concat_axis=1, tiled=True)
    dh = d_mixed_t.reshape(head_shape)
    d_prob = jnp.einsum("ctnhd,cunhd->cnhtu", dh, vh, preferred_element_type=jnp.float32)
    row_dot = jnp.sum(prob_full * d_prob, axis=-1, keepdims=True)
    d_scores = (prob_full * (d_prob - row_dot)).astype(jnp.bfloat16)
    column_shape = (clip_count, all_frames, column_tokens, channels)
    d_query = (
        (
            jnp.einsum("cnhtu,cunhd->ctnhd", d_scores, kh, preferred_element_type=jnp.float32)
            * scaling
        )
        .astype(jnp.bfloat16)
        .reshape(column_shape)
    )
    d_key = (
        (
            jnp.einsum("cnhtu,ctnhd->cunhd", d_scores, qh, preferred_element_type=jnp.float32)
            * scaling
        )
        .astype(jnp.bfloat16)
        .reshape(column_shape)
    )
    d_value = (
        jnp.einsum("cnhtu,ctnhd->cunhd", prob_half, dh, preferred_element_type=jnp.float32)
        .astype(jnp.bfloat16)
        .reshape(column_shape)
    )
    d_inputs_t = (
        project_back(d_query, w_query) + project_back(d_key, w_key) + project_back(d_value, w_value)
    ).astype(jnp.bfloat16)
    d_inputs = lax.all_to_all(d_inputs_t, "frame", split_axis=1, concat_axis=2, tiled=True)
    qkv_terms = [cross(latents_t, d_query), cross(latents_t, d_key), cross(latents_t, d_value)]
    grad_rows = (
        upstream.astype(jnp.float32) + d_inputs.reshape(-1, channels).astype(jnp.float32)
    ).astype(jnp.bfloat16)
    grad_input = grad_rows.reshape(clip_latents.shape)
    token_count = (
        clip_count
        * lax.axis_size("dp")
        * frame_count
        * lax.axis_size("frame")
        * pixels
        * lax.axis_size("height")
    )
    grad_scale = float(token_count) ** (-0.5)
    attn_term = jnp.concatenate(qkv_terms + [cross(mixed_rows, upstream)], axis=0) * grad_scale
    grad_attn = lax.psum_scatter(
        attn_term, ("frame", "height", "dp"), scatter_dimension=0, tiled=True
    )
    conv_term = jnp.concatenate(conv_terms, axis=0) * grad_scale
    owned = lax.psum_scatter(
        conv_term.astype(jnp.bfloat16), ("height", "dp"), scatter_dimension=0, tiled=True
    )
    grad_conv = over_copies(owned, "frame").astype(jnp.float32)
    return (grad_input, grad_attn, grad_conv)


def solution(mesh):
    in_specs = (
        P("dp", "frame", "height", None, None),
        P("dp", "frame", "height", None, None),
        P("dp", "frame", "height", None),
        P(),
        P(),
        P(),
    )
    out_specs = (
        P("dp", "frame", "height", None, None),
        P(("frame", "height", "dp"), None),
        P(("height", "dp"), None),
    )
    return jax.shard_map(body, mesh=mesh, in_specs=in_specs, out_specs=out_specs, check_vma=False)
```

profile of v0, /device:TPU:2, one launch (start us, length us, event | category | flops | bytes accessed | tf_op | source)
XLA Modules:
  0.0 555.3 jit_solution(17361230958055762102)
XLA Ops:
  9.0 1.4 copy.289
  10.4 1.3 pad_maximum_fusion.1
  11.7 10.3 %all-to-all-start = ((bf16[1,2,256,321]{3,1,0,2:T(2,128)(2,1)}), bf16[1,2,256,321]{3,1,0,2:T(2,128)(2,1)S(1)}, u32[]{:S(2)}, u32[]{:S(2)}) async-start(bf16[1,2,256,321]{3,1,0,2:T(2,128)(2,1)} %pad_maximum_fusion.1), calls=%async_computation | async-start | bytes 786432 | tf_op jit(solution)/shard_map/all_to_all | solution.py:13
  22.8 13.4 %all-to-all-done = bf16[1,2,256,321]{3,1,0,2:T(2,128)(2,1)S(1)} async-done(((bf16[1,2,256,321]{3,1,0,2:T(2,128)(2,1)}), bf16[1,2,256,321]{3,1,0,2:T(2,128)(2,1)S(1)}, u32[]{:S(2)}, u32[]{:S(2)}) %all-to-all-start) | async-done | bytes 328736 | tf_op jit(solution)/shard_map/all_to_all | solution.py:13
  38.7 1.4 reshape.291
  40.1 2.5 fusion.74
  42.6 2.3 fusion.7
  45.3 1.3 reshape.294
  46.6 4.8 all-to-all-start.1
  52.6 12.6 %all-to-all-done.1 = bf16[1,32,16,320]{3,2,0,1:T(8,128)(2,1)S(1)} async-done(((bf16[1,32,16,320]{3,2,0,1:T(8,128)(2,1)}), bf16[1,32,16,320]{3,2,0,1:T(8,128)(2,1)S(1)}, u32[]{:S(2)}, u32[]{:S(2)}) %all-to-all-start.1) | async-done | bytes 327712 | tf_op jit(solution)/shard_map/all_to_all | solution.py:108
  65.3 2.7 multiply_convert_fusion.2
  68.0 1.2 copy.308
  69.3 5.8 %collective-permute-start.1 = (bf16[1,2,1,16,640]{4,3,2,1,0:T(8,128)(2,1)S(1)}, bf16[1,2,1,16,640]{4,3,2,1,0:T(8,128)(2,1)S(1)}, u32[]{:S(2)}, u32[]{:S(2)}) collective-permute-start(bf16[1,2,1,16,640]{4,3,2,1,0:T(8,128)(2,1)S(1)} %get-tuple-element.36), channel_id=1, source_target_pairs={{2,0},{4,2},{6,4},{8,6},{10,8},{12,10},{14,12},{3,1},{5,3},{7,5},{... | collective-permute-start | bytes 122888 | tf_op jit(solution)/shard_map/ppermute | solution.py:32
  75.1 2.1 collective-permute-start
  78.5 4.6 collective-permute-done
  84.8 1.2 convolution_bitcast_fusion.8
  86.5 1.2 convolution_bitcast_fusion.7
  87.7 1.2 convolution_bitcast_fusion.6
  88.9 1.2 convolution_bitcast_fusion.5
  90.1 1.2 convolution_bitcast_fusion.3
  91.2 1.2 convolution_bitcast_fusion.2
  92.6 1.2 convolution_bitcast_fusion.1
  99.9 1.6 convolution_convert_fusion.5
  102.3 2.0 copy.309
  104.3 4.5 all-to-all-start.2
  109.2 4.7 concatenate.33
  113.9 3.7 multiply_convert_fusion
  117.6 3.3 all-to-all-done.2
  121.0 1.4 reshape.304
  122.5 2.9 multiply_reduce_fusion
  127.6 1.3 dot_general.138
  129.8 1.3 dot_general.141
  131.1 1.9 fusion.8
  133.4 1.3 dot_general.144
  134.8 1.5 fusion.46
  138.5 6.4 %all-to-all-start.3 = ((bf16[1,32,16,320]{3,2,0,1:T(8,128)(2,1)}), bf16[1,32,16,320]{3,2,0,1:T(8,128)(2,1)}, u32[]{:S(2)}, u32[]{:S(2)}) async-start(bf16[1,32,16,320]{3,2,0,1:T(8,128)(2,1)} %fusion.17), calls=%async_computation.3 | async-start | bytes 786432 | tf_op jit(solution)/shard_map/all_to_all | solution.py:181
  146.1 100.4 %all-reduce.8.cloned.1.call-done = bf16[2880,320]{0,1:T(8,128)(2,1)} async-done(((bf16[2880,320]{0,1:T(8,128)(2,1)}), bf16[2880,320]{0,1:T(8,128)(2,1)}) %all-reduce.8.cloned.1.call-update) | async-done | bytes 1843216
  246.5 1.7 constant_dynamic-slice_fusion
  248.2 1.7 copy.330
  249.9 2.5 broadcast_in_dim.2
  252.3 8.7 %all-to-all-start.4 = ((bf16[16,180,320]{2,1,0:T(8,128)(2,1)}), bf16[16,180,320]{2,1,0:T(8,128)(2,1)}, u32[]{:S(2)}, u32[]{:S(2)}) async-start(bf16[16,180,320]{2,1,0:T(8,128)(2,1)} %broadcast_in_dim.2), calls=%async_computation.4 | async-start | bytes 4521984 | tf_op jit(solution)/shard_map/all_to_all | solution.py:39
  261.3 2.2 fusion.82
  263.6 1.3 reshape_reshape.12
  264.9 1.3 reshape_reshape.13
  268.8 1.5 concatenate.32
  270.3 1.4 broadcast_multiply_fusion
  274.1 268.5 %all-reduce.6.cloned.1.call-done = f32[1280,320]{0,1:T(8,128)} async-done(((f32[1280,320]{0,1:T(8,128)}), f32[1280,320]{0,1:T(8,128)}) %all-reduce.6.cloned.1.call-update) | async-done | bytes 1638416
  544.4 3.4 convert_reduce_fusion
  (119 shorter events, 29.9 us)
Async XLA Ops:
  8.8 13.2 %copy-start.22 = (f32[5,32,32]{2,1,0:T(8,128)S(1)}, f32[5,32,32]{2,1,0:T(8,128)}, u32[]{:S(2)}) copy-start(f32[5,32,32]{2,1,0:T(8,128)} %param.11) | copy-start | bytes 61444
  11.7 24.6 %copy-start.18 = (bf16[1280,320]{0,1:T(8,128)(2,1)S(1)}, bf16[1280,320]{0,1:T(8,128)(2,1)}, u32[]{:S(2)}) copy-start(bf16[1280,320]{0,1:T(8,128)(2,1)} %param.9) | copy-start | bytes 2457604
  11.7 24.4 %all-to-all-start = ((bf16[1,2,256,321]{3,1,0,2:T(2,128)(2,1)}), bf16[1,2,256,321]{3,1,0,2:T(2,128)(2,1)S(1)}, u32[]{:S(2)}, u32[]{:S(2)}) async-start(bf16[1,2,256,321]{3,1,0,2:T(2,128)(2,1)} %pad_maximum_fusion.1), calls=%async_computation | async-start | bytes 786432 | tf_op jit(solution)/shard_map/all_to_all | solution.py:13
  38.3 1.8 copy-start.3
  38.3 1.8 copy-start.23
  42.6 2.3 copy-start.24
  45.3 6.2 %copy-start.11 = (bf16[1,2,16,16,320]{4,3,2,1,0:T(8,128)(2,1)S(1)}, bf16[1,2,16,16,320]{4,3,2,1,0:T(8,128)(2,1)}, u32[]{:S(2)}) copy-start(bf16[1,2,16,16,320]{4,3,2,1,0:T(8,128)(2,1)} %param.6) | copy-start | bytes 983044
  45.3 7.2 %copy-start = (bf16[1,2,16,16,320]{4,3,2,1,0:T(8,128)(2,1)S(1)}, bf16[1,2,16,16,320]{4,3,2,1,0:T(8,128)(2,1)}, u32[]{:S(2)}) copy-start(bf16[1,2,16,16,320]{4,3,2,1,0:T(8,128)(2,1)} %param.7) | copy-start | bytes 983044
  46.6 18.6 %all-to-all-start.1 = ((bf16[1,32,16,320]{3,2,0,1:T(8,128)(2,1)}), bf16[1,32,16,320]{3,2,0,1:T(8,128)(2,1)S(1)}, u32[]{:S(2)}, u32[]{:S(2)}) async-start(bf16[1,32,16,320]{3,2,0,1:T(8,128)(2,1)} %bitcast.233), calls=%async_computation.1 | async-start | bytes 786432 | tf_op jit(solution)/shard_map/all_to_all | solution.py:108
  65.3 2.7 copy-start.12
  68.0 10.4 %copy-start.21 = (f32[2,256,320]{1,2,0:T(8,128)S(1)}, f32[2,256,320]{1,2,0:T(8,128)}, u32[]{:S(2)}) copy-start(f32[2,256,320]{1,2,0:T(8,128)} %get-tuple-element.40) | copy-start | bytes 1966084
  69.3 9.2 %collective-permute-start.1 = (bf16[1,2,1,16,640]{4,3,2,1,0:T(8,128)(2,1)S(1)}, bf16[1,2,1,16,640]{4,3,2,1,0:T(8,128)(2,1)S(1)}, u32[]{:S(2)}, u32[]{:S(2)}) collective-permute-start(bf16[1,2,1,16,640]{4,3,2,1,0:T(8,128)(2,1)S(1)} %get-tuple-element.36), channel_id=1, source_target_pairs={{2,0},{4,2},{6,4},{8,6},{10,8},{12,10},{14,12},{3,1},{5,3},{7,5},{... | collective-permute-start | bytes 122888 | tf_op jit(solution)/shard_map/ppermute | solution.py:32
  75.1 8.0 %collective-permute-start = (bf16[1,2,1,16,640]{4,3,2,1,0:T(8,128)(2,1)S(1)}, bf16[1,2,1,16,640]{4,3,2,1,0:T(8,128)(2,1)S(1)}, u32[]{:S(2)}, u32[]{:S(2)}) collective-permute-start(bf16[1,2,1,16,640]{4,3,2,1,0:T(8,128)(2,1)S(1)} %get-tuple-element.35), channel_id=1, source_target_pairs={{0,2},{2,4},{4,6},{6,8},{8,10},{10,12},{12,14},{1,3},{3,5},{5,7},{... | collective-permute-start | bytes 122888 | tf_op jit(solution)/shard_map/ppermute | solution.py:29
  92.6 2.4 copy-start.5
  99.2 0.7 copy-start.1
  99.9 9.2 %copy-start.7 = (f32[320,320]{0,1:T(8,128)S(1)}, f32[320,320]{0,1:T(8,128)}, u32[]{:S(2)}) copy-start(f32[320,320]{0,1:T(8,128)} %convolution_bitcast_fusion.4) | copy-start | bytes 1228804
  99.9 9.2 %copy-start.8 = (f32[320,320]{0,1:T(8,128)S(1)}, f32[320,320]{0,1:T(8,128)}, u32[]{:S(2)}) copy-start(f32[320,320]{0,1:T(8,128)} %convolution_bitcast_fusion.8) | copy-start | bytes 1228804
  99.9 9.2 %copy-start.9 = (f32[320,320]{0,1:T(8,128)S(1)}, f32[320,320]{0,1:T(8,128)}, u32[]{:S(2)}) copy-start(f32[320,320]{0,1:T(8,128)} %convolution_bitcast_fusion.7) | copy-start | bytes 1228804
  104.3 16.6 %all-to-all-start.2 = ((bf16[1,2,256,320]{3,1,0,2:T(2,128)(2,1)}), bf16[1,2,256,320]{3,1,0,2:T(2,128)(2,1)S(1)}, u32[]{:S(2)}, u32[]{:S(2)}) async-start(bf16[1,2,256,320]{3,1,0,2:T(2,128)(2,1)} %copy.309), calls=%async_computation.2 | async-start | bytes 786432 | tf_op jit(solution)/shard_map/all_to_all | solution.py:151
  108.9 137.6 %all-reduce.8.cloned.1.call-start = ((), (), s32[]{:S(2)}) async-start(), calls=%async_computation.6 | async-start | bytes 3768320
  120.9 1.5 copy-start.16
  120.9 1.5 copy-start.25
  122.5 2.9 copy-start.17
  125.3 1.2 copy-start.4
  129.5 1.7 copy-start.20
  134.8 1.6 copy-start.15
  134.8 1.6 copy-start.19
  136.3 1.0 copy-start.10
  137.3 7.5 %copy-start.26 = (u32[256]{0:T(256)S(1)}, u32[256]{0:T(256)}, u32[]{:S(2)}) copy-start(u32[256]{0:T(256)} %constant.30) | copy-start | bytes 3076
  138.5 111.4 %all-to-all-start.3 = ((bf16[1,32,16,320]{3,2,0,1:T(8,128)(2,1)}), bf16[1,32,16,320]{3,2,0,1:T(8,128)(2,1)}, u32[]{:S(2)}, u32[]{:S(2)}) async-start(bf16[1,32,16,320]{3,2,0,1:T(8,128)(2,1)} %fusion.17), calls=%async_computation.3 | async-start | bytes 786432 | tf_op jit(solution)/shard_map/all_to_all | solution.py:181
  252.3 292.1 %all-to-all-start.4 = ((bf16[16,180,320]{2,1,0:T(8,128)(2,1)}), bf16[16,180,320]{2,1,0:T(8,128)(2,1)}, u32[]{:S(2)}, u32[]{:S(2)}) async-start(bf16[16,180,320]{2,1,0:T(8,128)(2,1)} %broadcast_in_dim.2), calls=%async_computation.4 | async-start | bytes 4521984 | tf_op jit(solution)/shard_map/all_to_all | solution.py:39
  261.0 281.6 %all-reduce.6.cloned.1.call-start = ((), (), s32[]{:S(2)}) async-start(), calls=%async_computation.5 | async-start | bytes 3276800
  264.9 1.9 copy-start.13
  266.2 1.0 copy-start.14
  267.2 1.6 copy-start.6
  271.7 1.4 copy-start.2
Sparse Core Ops, SparseCore 0:
  117.7 128.7 all-reduce.7
Sparse Core Ops, SparseCore 1:
  271.8 270.8 all-reduce.5
where the time goes:
time: 557 us; the launch traced here: 555 us
  waiting for transfers between devices  403 us (72%)
  starting transfers between devices  43.1 us (8%)
  local copies, waits for them, and re-layouts  41.8 us (8%)
  matrix products  38.5 us (7%)
  between operations  16.8 us (3%)
  other arithmetic  12.3 us (2%)
    unnamed x4, waiting for transfers between devices  369 us
    dot_general x13, matrix products, cross(): lax.dot_general(left_rows, right_rows, (((0,), (0,)), ((), ())), preferre...  14.8 us
    all_to_all x1, waiting for transfers between devices, side_by_side(): lax.all_to_all(both, axis, split_axis=split_dim, concat_axis=concat_dim,...  13.4 us
    all_to_all x1, waiting for transfers between devices, body(): lax.all_to_all(mixed_t, 'frame', split_axis=1, concat_axis=2, tiled=True)  12.6 us
  transfers between devices with their start and end apart: 9, of which 6 were waited for; matrix products, arithmetic and copies ran while one was open for 8% of the time, Pallas kernels for 0%

commit v1 on v0

v1 whole, which is shorter than its diff:
```python
import jax
import jax.numpy as jnp
from jax import lax
from jax.experimental import pallas as pl
from jax.experimental.pallas import tpu as pltpu
from jax.sharding import PartitionSpec as P

F32 = jnp.float32
BF16 = jnp.bfloat16
GROUND_BIAS = 2.0
NF, NH, ND = 16, 8, 2
C = 320
CP = 384
HEADS = 5
T = 32
W = 16
ROWS = T * W
BLK = 128
NB = ROWS // BLK
NEG = -1e30
TOKENS = 2 * 32 * 128 * 16
GRAD_SCALE = float(TOKENS) ** -0.5
SCALING = 0.125


def peer(**where):
    return dict(device_id=where, device_id_type=pl.DeviceIdType.MESH)


def gather_kernel(x_ref, dy_ref, xt_ref, dy0_ref, dyu_ref, dyd_ref, xs, xr, ds, dr, hs, hr, ls):
    f = lax.axis_index("frame")
    h = lax.axis_index("height")
    lin = h * NF + f
    prev = lax.rem(lin + NF * NH - 1, NF * NH)
    nxt = lax.rem(lin + 1, NF * NH)
    barrier = pltpu.get_barrier_semaphore()
    for k in range(1, NF):
        pl.semaphore_signal(barrier, inc=1, **peer(frame=lax.rem(f + k, NF)))

    @pl.when(f == 0)
    def _():
        pl.semaphore_signal(barrier, inc=1, **peer(frame=lax.rem(prev, NF), height=prev // NF))

    @pl.when(f == NF - 1)
    def _():
        pl.semaphore_signal(barrier, inc=1, **peer(frame=lax.rem(nxt, NF), height=nxt // NF))

    edge = jnp.where(jnp.logical_or(f == 0, f == NF - 1), 1, 0)
    pl.semaphore_wait(barrier, NF - 1 + edge)

    def sends(src, dst, ssem, rsem):
        out = []
        for k in range(1, NF):
            p = lax.rem(f + k, NF)
            cp = pltpu.make_async_remote_copy(
                src_ref=src.at[:, p],
                dst_ref=dst.at[pl.ds(2 * f, 2)],
                send_sem=ssem.at[k],
                recv_sem=rsem.at[k],
                **peer(frame=p),
            )
            cp.start()
            out.append(cp)
        return out

    xc = sends(x_ref, xt_ref, xs, xr)
    dc = sends(dy_ref, dy0_ref, ds, dr)
    lx = pltpu.make_async_copy(x_ref.at[:, f], xt_ref.at[pl.ds(2 * f, 2)], ls.at[0])
    ld = pltpu.make_async_copy(dy_ref.at[:, f], dy0_ref.at[pl.ds(2 * f, 2)], ls.at[1])
    lx.start()
    ld.start()
    lx.wait()
    ld.wait()
    for cp in xc:
        cp.wait_recv()
    for cp in dc:
        cp.wait_recv()
    up = pltpu.make_async_remote_copy(
        src_ref=dy0_ref,
        dst_ref=dyd_ref,
        send_sem=hs.at[0],
        recv_sem=hr.at[0],
        **peer(frame=lax.rem(prev, NF), height=prev // NF),
    )
    down = pltpu.make_async_remote_copy(
        src_ref=dy0_ref,
        dst_ref=dyu_ref,
        send_sem=hs.at[1],
        recv_sem=hr.at[1],
        **peer(frame=lax.rem(nxt, NF), height=nxt // NF),
    )
    up.start()
    down.start()
    for cp in xc + dc:
        cp.wait_send()
    up.wait()
    down.wait()


def gather_rows(x_aug, dy):
    vm = pl.BlockSpec(memory_space=pltpu.VMEM)
    row = jax.ShapeDtypeStruct((T, W, C), BF16)
    dma = pltpu.SemaphoreType.DMA
    return pl.pallas_call(
        gather_kernel,
        out_shape=(jax.ShapeDtypeStruct((T, W, CP), BF16), row, row, row),
        in_specs=[vm, vm],
        out_specs=(vm, vm, vm, vm),
        scratch_shapes=[dma((NF,)), dma((NF,)), dma((NF,)), dma((NF,)), dma((2,)), dma((2,)), dma((2,))],
        compiler_params=pltpu.CompilerParams(collective_id=0, has_side_effects=True),
        name="gather_rows",
    )(x_aug, dy)


def nn(a, b):
    return lax.dot_general(a, b, (((1,), (0,)), ((), ())), preferred_element_type=F32)


def nt(a, b):
    return lax.dot_general(a, b, (((1,), (1,)), ((), ())), preferred_element_type=F32)


def tn(a, b):
    return lax.dot_general(a, b, (((0,), (0,)), ((), ())), preferred_element_type=F32)


def pixel_major(src, tr, store, width):
    for s in range(0, width, 128):
        w = min(128, width - s)
        tr[s // 128, :, :w] = src[:, :, s : s + w].reshape(ROWS, w).astype(F32)
    for p in range(W):
        for s in range(0, width, 128):
            w = min(128, width - s)
            store(p, s, w, tr[s // 128, pl.ds(p, T, stride=W), :][:, :w].astype(BF16))


def compute_kernel(
    xt_ref, dy0_ref, dyu_ref, dyd_ref, wa_ref, wc_ref, tb_ref,
    gi_ref, attn_ref, conv_ref,
    tr, xp, dyp, q_s, k_s, v_s, o_s, pr, bias_s, y1_s, a_t, da_s, g_s, do_s, dq_s, dk_s, dv_s, x_t, o_t, cf,
):
    lin = lax.axis_index("height") * NF + lax.axis_index("frame")

    def put_x(p, s, w, val):
        xp[p * T : (p + 1) * T, s : s + w] = val

    pixel_major(xt_ref, tr, put_x, CP)
    x = xp[:, :C]
    q_s[...] = nn(x, wa_ref[0:C]).astype(BF16)
    k_s[...] = nn(x, wa_ref[C : 2 * C]).astype(BF16)
    v_s[...] = nn(x, wa_ref[2 * C : 3 * C]).astype(BF16)

    ri = lax.broadcasted_iota(jnp.int32, (BLK, BLK), 0) // T
    ci = lax.broadcasted_iota(jnp.int32, (BLK, BLK), 1) // T
    for hd in range(HEADS):
        one = tb_ref[hd]
        wide = jnp.concatenate([one] * 4, axis=1)
        full = jnp.concatenate([wide] * 4, axis=0)
        bias_s[hd] = jnp.where(ri == ci, full, NEG)
    lane = lax.broadcasted_iota(jnp.int32, (BLK, 128), 1)
    low = lane < 64
    ones = jnp.full((8, 128), GROUND_BIAS, BF16)

    slabs = ((0, 128, (0, 1)), (128, 128, (2, 3)), (256, 64, (4,)))

    def only(val, i, w):
        if w == 64:
            return val
        keep = low if i == 0 else jnp.logical_not(low)
        return jnp.where(keep, val, jnp.zeros_like(val))

    def pick(parts, w):
        if w == 64:
            return parts[0]
        return jnp.where(low, parts[0], parts[1])

    for b in range(NB):
        rows = slice(b * BLK, (b + 1) * BLK)
        marks = jnp.where(lane == 64, xp[rows, 256:384], jnp.zeros((BLK, 128), BF16))
        key_bias = nt(ones, marks)[0:1, :]
        for s, w, heads in slabs:
            ls = slice(s, s + w)
            qb, kb, vb = q_s[rows, ls], k_s[rows, ls], v_s[rows, ls]
            outs = []
            for i, hd in enumerate(heads):
                sc = nt(only(qb, i, w), kb) * SCALING + bias_s[hd] + key_bias
                e = jnp.exp(sc - jnp.max(sc, axis=-1, keepdims=True))
                pf = e / jnp.sum(e, axis=-1, keepdims=True)
                pr[b, hd] = pf
                outs.append(nn(pf.astype(BF16), vb))
            o_s[rows, ls] = pick(outs, w).astype(BF16)

    y1 = (x.astype(F32) + nn(o_s[...], wa_ref[3 * C :])).astype(BF16)
    y1_s[...] = y1
    yf = y1.astype(F32)
    act = yf / (1.0 + jnp.exp(-yf))
    a_t[...] = act.T.astype(BF16)
    x_t[...] = x.astype(F32).T.astype(BF16)
    o_t[...] = o_s[...].astype(F32).T.astype(BF16)

    zero = jnp.zeros((T, C), BF16)
    for r, (src, keep) in enumerate(((dyd_ref, lin < NF * NH - 1), (dy0_ref, None), (dyu_ref, lin > 0))):
        dyp[r, 0:T, :] = zero
        dyp[r, (W + 1) * T :, :] = zero

        def put(p, s, w, val, r=r, keep=keep):
            if keep is not None:
                val = jnp.where(keep, val, jnp.zeros_like(val))
            dyp[r, (p + 1) * T : (p + 2) * T, s : s + w] = val

        pixel_major(src, tr, put, C)

    first = True
    for r in range(3):
        for c in range(3):
            tap = 3 * r + c
            off = (2 - c) * T
            shifted = dyp[r, off : off + ROWS, :]
            taps = slice(tap * C, (tap + 1) * C)
            part = nt(shifted, wc_ref[taps])
            da_s[...] = part if first else da_s[...] + part
            first = False
            cf[taps, :] = nn(a_t[...], shifted) * GRAD_SCALE
    for k in range(NH * ND):
        conv_ref[k // ND, k % ND] = cf[k * 180 : (k + 1) * 180, :].astype(BF16)

    yf = y1_s[...].astype(F32)
    sig = 1.0 / (1.0 + jnp.exp(-yf))
    slope = sig * (1.0 + yf * (1.0 - sig))
    g = (dyp[1, T : T + ROWS, :].astype(F32) + slope * da_s[...]).astype(BF16)
    g_s[...] = g
    do_s[...] = nt(g, wa_ref[3 * C :]).astype(BF16)

    for b in range(NB):
        rows = slice(b * BLK, (b + 1) * BLK)
        for s, w, heads in slabs:
            ls = slice(s, s + w)
            qb, kb, vb, db = q_s[rows, ls], k_s[rows, ls], v_s[rows, ls], do_s[rows, ls]
            dqs, dks, dvs = [], [], []
            for i, hd in enumerate(heads):
                pf = pr[b, hd]
                dp = nt(only(db, i, w), vb)
                dsc = (pf * (dp - jnp.sum(pf * dp, axis=-1, keepdims=True)))
                dsc = dsc.astype(BF16)
                dqs.append(nn(dsc, kb))
                dks.append(tn(dsc, qb))
                dvs.append(tn(pf.astype(BF16), db))
            dq_s[rows, ls] = (pick(dqs, w) * SCALING).astype(BF16)
            dk_s[rows, ls] = (pick(dks, w) * SCALING).astype(BF16)
            dv_s[rows, ls] = pick(dvs, w).astype(BF16)

    dx = nt(dq_s[...], wa_ref[0:C]) + nt(dk_s[...], wa_ref[C : 2 * C]) + nt(dv_s[...], wa_ref[2 * C : 3 * C])
    gi = g_s[...].astype(F32) + dx.astype(BF16).astype(F32)
    for s in range(0, C, 128):
        w = min(128, C - s)
        tr[s // 128, :, :w] = gi[:, s : s + w]
    for t in range(T):
        for s in range(0, C, 128):
            w = min(128, C - s)
            gi_ref[t, :, s : s + w] = tr[s // 128, pl.ds(t, W, stride=T), :][:, :w].astype(BF16)

    for j, (left, right) in enumerate(((x_t, dq_s), (x_t, dk_s), (x_t, dv_s), (o_t, g_s))):
        term = (nn(left[...], right[...]) * GRAD_SCALE).astype(F32)
        for k in range(8):
            m = 8 * j + k
            attn_ref[m // 2, m % 2] = term[40 * k : 40 * (k + 1), :].astype(BF16)


def compute(xt, dy0, dyu, dyd, wa, wc, tb):
    vm = pl.BlockSpec(memory_space=pltpu.VMEM)
    v = pltpu.VMEM
    tok = v((ROWS, C), BF16)
    return pl.pallas_call(
        compute_kernel,
        out_shape=(
            jax.ShapeDtypeStruct((T, W, C), BF16),
            jax.ShapeDtypeStruct((NF, ND, 40, C), BF16),
            jax.ShapeDtypeStruct((NH, ND, 180, C), BF16),
        ),
        in_specs=[vm] * 7,
        out_specs=(vm, vm, vm),
        scratch_shapes=[
            v((3, ROWS, 128), F32), v((ROWS, CP), BF16), v((3, ROWS + 2 * T, C), BF16),
            tok, tok, tok, tok,
            v((NB, HEADS, BLK, BLK), F32), v((HEADS, BLK, BLK), F32),
            tok, v((C, ROWS), BF16), v((ROWS, C), F32), tok, tok, tok, tok, tok,
            v((C, ROWS), BF16), v((C, ROWS), BF16), v((9 * C, C), F32),
        ],
        name="block_backward",
    )(xt, dy0, dyu, dyd, wa, wc, tb)


def scatter_kernel(
    gi_ref, attn_ref, conv_ref,
    out_ref, oattn_ref, oconv_ref,
    conv_a, attn_a, conv_1, attn_1, conv_b, attn_b, conv_f, conv_c, conv_cr, conv_d, conv_dr, attn_c, attn_cr,
    gs, gr, pa, pb, cs, cr, as_, ar, c2s, c2r, c3s, c3r, a2s, a2r, lsem,
):
    f = lax.axis_index("frame")
    h = lax.axis_index("height")
    d = lax.axis_index("dp")
    other = 1 - d
    me = h * ND + d
    barrier = pltpu.get_barrier_semaphore()
    for k in range(1, NF):
        pl.semaphore_signal(barrier, inc=1, **peer(frame=lax.rem(f + k, NF)))
    for k in range(1, NH * ND):
        q = lax.rem(me + k, NH * ND)
        pl.semaphore_signal(barrier, inc=1, **peer(height=q // ND, dp=lax.rem(q, ND)))
    pl.semaphore_wait(barrier, NF + NH * ND - 2)

    def remote(src, dst, ss, rs, **where):
        cp = pltpu.make_async_remote_copy(src_ref=src, dst_ref=dst, send_sem=ss, recv_sem=rs, **peer(**where))
        cp.start()
        return cp

    ca = remote(conv_ref.at[:, other], conv_a, pa.at[0], pb.at[0], dp=other)
    aa = remote(attn_ref.at[:, other], attn_a, pa.at[1], pb.at[1], dp=other)
    gic = []
    for k in range(1, NF):
        p = lax.rem(f + k, NF)
        gic.append(remote(gi_ref.at[pl.ds(2 * p, 2)], out_ref.at[:, f], gs.at[k], gr.at[k], frame=p))
    own = pltpu.make_async_copy(gi_ref.at[pl.ds(2 * f, 2)], out_ref.at[:, f], lsem.at[0])
    own.start()

    ca.wait_recv()
    for j in range(NH):
        conv_1[j] = (conv_ref[j, d].astype(F32) + conv_a[j].astype(F32)).astype(BF16)
    cc = []
    for k in range(1, NH):
        p = lax.rem(h + k, NH)
        cc.append(remote(conv_1.at[p], conv_b.at[k], cs.at[k], cr.at[k], height=p))
    aa.wait_recv()
    for j in range(NF):
        attn_1[j] = (attn_ref[j, d].astype(F32) + attn_a[j].astype(F32)).astype(BF16)
    ac = []
    for k in range(1, NF):
        p = lax.rem(f + k, NF)
        ac.append(remote(attn_1.at[p], attn_b.at[k], as_.at[k], ar.at[k], frame=p))

    total = attn_1[f].astype(F32)
    for k in range(1, NF):
        ac[k - 1].wait_recv()
        total = total + attn_b[k].astype(F32)
    for j in range(8):
        attn_c[j] = total[5 * j : 5 * j + 5, :]
    half = h // 4
    a2 = []
    for j in range(8):
        th, td = 4 * d + j // 2, j % 2
        mine = jnp.logical_and(th == h, td == d)

        @pl.when(jnp.logical_not(mine))
        def _(j=j, th=th, td=td):
            remote(attn_c.at[j], attn_cr.at[h], a2s.at[j], a2r.at[h], height=th, dp=td)

        @pl.when(mine)
        def _(j=j):
            attn_cr[h] = attn_c[j]

    total = conv_1[h].astype(F32)
    for k in range(1, NH):
        cc[k - 1].wait_recv()
        total = total + conv_b[k].astype(F32)
    conv_f[0:180, :] = total
    conv_f[180:192, :] = jnp.zeros((12, C), F32)
    for j in range(NF):
        conv_c[j] = conv_f[12 * j : 12 * j + 12, :].astype(BF16)
    c2 = []
    for k in range(1, NF):
        p = lax.rem(f + k, NF)
        c2.append(remote(conv_c.at[p], conv_cr.at[k], c2s.at[k], c2r.at[k], frame=p))
    total = conv_c[f].astype(F32)
    for k in range(1, NF):
        c2[k - 1].wait_recv()
        total = total + conv_cr[k].astype(F32)
    conv_d[...] = total.astype(BF16)
    c3 = []
    for k in range(1, NF):
        p = lax.rem(f + k, NF)
        c3.append(remote(conv_d, conv_dr.at[f], c3s.at[k], c3r.at[k], frame=p))
    conv_dr[f] = total.astype(BF16)

    def arrived(i):
        return pltpu.make_async_remote_copy(
            src_ref=attn_c.at[0], dst_ref=attn_cr.at[i], send_sem=a2s.at[i], recv_sem=a2r.at[i], **peer(dp=other)
        )

    for i in range(8):
        @pl.when(jnp.logical_not(jnp.logical_and(i == h, d == half)))
        def _(i=i):
            arrived(i).wait_recv()

    total = attn_cr[0]
    for i in range(1, 8):
        total = total + attn_cr[i]
    oattn_ref[...] = total

    for cp in c3:
        cp.wait_recv()
    for j in range(NF - 1):
        oconv_ref[12 * j : 12 * j + 12, :] = conv_dr[j].astype(F32)
    own.wait()
    for cp in gic:
        cp.wait_recv()
    for cp in [ca, aa] + gic + cc + ac + c2 + c3:
        cp.wait_send()
    for j in range(8):
        th, td = 4 * d + j // 2, j % 2

        @pl.when(jnp.logical_not(jnp.logical_and(th == h, td == d)))
        def _(j=j):
            arrived(j).wait_send()


def scatter_results(gi, attn, conv):
    vm = pl.BlockSpec(memory_space=pltpu.VMEM)
    v = pltpu.VMEM
    dma = pltpu.SemaphoreType.DMA
    return pl.pallas_call(
        scatter_kernel,
        out_shape=(
            jax.ShapeDtypeStruct((2, W, W, C), BF16),
            jax.ShapeDtypeStruct((5, C), F32),
            jax.ShapeDtypeStruct((180, C), F32),
        ),
        in_specs=[vm] * 3,
        out_specs=(vm, vm, vm),
        scratch_shapes=[
            v((NH, 180, C), BF16), v((NF, 40, C), BF16), v((NH, 180, C), BF16), v((NF, 40, C), BF16),
            v((NH, 180, C), BF16), v((NF, 40, C), BF16), v((192, C), F32), v((NF, 12, C), BF16), v((NF, 12, C), BF16),
            v((12, C), BF16), v((NF, 12, C), BF16), v((8, 5, C), F32), v((8, 5, C), F32),
            dma((NF,)), dma((NF,)), dma((2,)), dma((2,)), dma((NH,)), dma((NH,)), dma((NF,)), dma((NF,)),
            dma((NF,)), dma((NF,)), dma((NF,)), dma((NF,)), dma((8,)), dma((8,)), dma((1,)),
        ],
        compiler_params=pltpu.CompilerParams(collective_id=1, has_side_effects=True),
        name="scatter_results",
    )(gi, attn, conv)


def body(clip_latents, out_grad, box_mask, attn_weights, conv_weights, time_bias):
    x = clip_latents[0]
    dy = out_grad[0]
    marks = box_mask[0][..., None].astype(BF16)
    x_aug = jnp.concatenate([x, marks, jnp.zeros(x.shape[:3] + (CP - C - 1,), BF16)], axis=-1)
    xt, dy0, dyu, dyd = gather_rows(x_aug, dy)
    gi, attn, conv = compute(xt, dy0, dyu, dyd, attn_weights, conv_weights, time_bias)
    out, oattn, oconv = scatter_results(gi, attn, conv)
    return out[None], oattn, oconv


def solution(mesh):
    in_specs = (
        P("dp", "frame", "height", None, None),
        P("dp", "frame", "height", None, None),
        P("dp", "frame", "height", None),
        P(),
        P(),
        P(),
    )
    out_specs = (
        P("dp", "frame", "height", None, None),
        P(("frame", "height", "dp"), None),
        P(("height", "dp"), None),
    )
    return jax.shard_map(body, mesh=mesh, in_specs=in_specs, out_specs=out_specs, check_vma=False)
```

time: 557 us -> 132 us (0.24)
  waiting for transfers between devices: 403 us -> 0 us
  Pallas kernels: 0 us -> 117 us
  starting transfers between devices: 43.1 us -> 0 us
  matrix products: 38.5 us -> 0 us
  local copies, waits for them, and re-layouts: 41.8 us -> 10 us
  between operations: 16.8 us -> 0.67 us
  other arithmetic: 12.3 us -> 2.71 us
    unnamed x4 -> x0, waiting for transfers between devices: 369 us -> none
    pallas_call x0 -> x3, Pallas kernels: none -> 117 us  [the longest x1 49.9 us: scatter_results(): pl.pallas_call(scatter_kernel, out_shape=(jax.ShapeDtypeStruct((2, W, W,...]
    dot_general x35 -> x0, matrix products: 36 us -> none  [the longest x13 14.8 us: cross(): lax.dot_general(left_rows, right_rows, (((0,), (0,)), ((), ())), preferre...]
    all_to_all x5 -> x0, starting transfers between devices: 34.7 us -> none  [the longest x1 10.3 us: side_by_side(): lax.all_to_all(both, axis, split_axis=split_dim, concat_axis=concat_dim,...]
    all_to_all x5 -> x0, waiting for transfers between devices: 29.3 us -> none  [the longest x1 13.4 us: side_by_side(): lax.all_to_all(both, axis, split_axis=split_dim, concat_axis=concat_dim,...]
    ppermute x2 -> x0, starting transfers between devices: 7.89 us -> none  [the longest x1 5.79 us: padded_2(): lax.ppermute(lax.slice_in_dim(block, 0, width, axis=dim), axis, backward)]
    another operation x6 -> x0, local copies, waits for them, and re-layouts: 6.37 us -> none
    concatenate x2 -> x1, local copies, waits for them, and re-layouts: 6.26 us -> 0.08 us  [body(): jnp.concatenate([x, marks, jnp.zeros(x.shape[:3] + (CP - C - 1,), BF16)],...]
  transfers between devices with their start and end apart: 9 -> 0, of which waited for: 6 -> 0; matrix products, arithmetic and copies ran while one was open for 8% -> 0% of each run, Pallas kernels for 0% -> 0%
where the time goes in v1:
time: 132 us; the launch traced here: 131 us
  Pallas kernels  117 us (89%)
  local copies, waits for them, and re-layouts  10 us (8%)
  other arithmetic  2.71 us (2%)
    pallas_call x1, Pallas kernels, scatter_results(): pl.pallas_call(scatter_kernel, out_shape=(jax.ShapeDtypeStruct((2, W, W,...  49.9 us
    pallas_call x1, Pallas kernels, gather_rows(): pl.pallas_call(gather_kernel, out_shape=(jax.ShapeDtypeStruct((T, W, CP),...  44.4 us
    pallas_call x1, Pallas kernels, compute(): pl.pallas_call(compute_kernel, out_shape=(jax.ShapeDtypeStruct((T, W, C),...  22.8 us
    unnamed x7, local copies, waits for them, and re-layouts  9.65 us

profile of v1, /device:TPU:2, one launch (start us, length us, event | category | flops | bytes accessed | tf_op | source)
XLA Modules:
  0.0 130.6 jit_solution(4061267291870613093)
XLA Ops:
  0.6 0.0 copy-start
  0.7 0.1 pad.2.clone
  0.7 0.8 convert_bitcast_fusion
  1.6 0.3 copy.11
  1.9 1.9 %maximum_maximum_fusion.x_ref = bf16[2,16,16,384]{3,2,1,0:T(8,128)(2,1)} fusion(bf16[2,16,16,1]{3,2,1,0:T(8,128)(2,1)S(1)} %copy.11, bf16[2,16,16,320]{3,2,1,0:T(8,128)(2,1)} %bitcast.5, bf16[384]{0:T(512)(128)(2,1)S(1)} %pad.2.clone), kind=kLoop, calls=%fused_computation | loop fusion | flops 1179648 | bytes 722688 | tf_op jit(solution)/shard_map/concatenate | solution.py:445
  3.7 2.2 %copy.12.wa_ref = bf16[1280,320]{1,0:T(8,128)(2,1)} copy(bf16[1280,320]{0,1:T(8,128)(2,1)} %param.9) | data formatting | bytes 1638400 | tf_op args[3]
  5.9 44.4 %gather_rows.1 = (bf16[32,16,384]{2,1,0:T(8,128)(2,1)}, bf16[32,16,320]{2,1,0:T(8,128)(2,1)}, bf16[32,16,320]{2,1,0:T(8,128)(2,1)}, bf16[32,16,320]{2,1,0:T(8,128)(2,1)}) custom-call(bf16[2,16,16,384]{3,2,1,0:T(8,128)(2,1)} %maximum_maximum_fusion.x_ref, bf16[2,16,16,320]{3,2,1,0:T(8,128)(2,1)} %bitcast.6), custom_call_target="tpu_custom_call" | custom-call | tf_op jit(solution)/shard_map/gather_rows/pallas_call | solution.py:104
  50.3 0.0 copy-done
  50.4 2.7 %copy.13.wc_ref = bf16[2880,320]{1,0:T(8,128)(2,1)} copy(bf16[2880,320]{0,1:T(8,128)(2,1)S(1)} %copy-done) | data formatting | bytes 3686400 | tf_op args[4]
  53.0 22.8 %block_backward.1 = (bf16[32,16,320]{2,1,0:T(8,128)(2,1)}, bf16[16,2,40,320]{3,2,1,0:T(8,128)(2,1)}, bf16[8,2,180,320]{3,2,1,0:T(8,128)(2,1)}) custom-call(bf16[32,16,384]{2,1,0:T(8,128)(2,1)} %get-tuple-element.13.xt_ref, bf16[32,16,320]{2,1,0:T(8,128)(2,1)} %get-tuple-element.14.dy0_ref, bf16[32,16,320]{2,1,0:T(8,128)(2,1)} %get-tuple-element.15.dyu_ref, ...), custom_call_target="tpu_custom_call" | custom-call | tf_op jit(solution)/shard_map/block_backward/pallas_call | solution.py:273
  75.9 49.9 %scatter_results.1 = (bf16[2,16,16,320]{3,2,1,0:T(8,128)(2,1)}, f32[5,320]{1,0:T(8,128)}, f32[180,320]{1,0:T(8,128)}) custom-call(bf16[32,16,320]{2,1,0:T(8,128)(2,1)} %get-tuple-element.17.gi_ref, bf16[16,2,40,320]{3,2,1,0:T(8,128)(2,1)} %get-tuple-element.18.attn_ref, bf16[8,2,180,320]{3,2,1,0:T(8,128)(2,1)} %get-tuple-element.19.conv_ref), custom_call_target="tpu_custom_call" | custom-call | tf_op jit(solution)/shard_map/scatter_results/pallas_call | solution.py:420
  125.8 1.8 %copy.17 = bf16[1,2,16,16,320]{4,3,2,1,0:T(8,128)(2,1)} copy(bf16[1,2,16,16,320]{4,3,2,1,0:T(8,128)(2,1)} %bitcast.7) | data formatting | bytes 655360
  127.6 1.3 %copy.18 = f32[5,320]{1,0:T(8,128)} copy(f32[5,320]{1,0:T(8,128)} %get-tuple-element.27) | data formatting | bytes 12800
  128.9 1.7 %copy.19 = f32[180,320]{1,0:T(8,128)} copy(f32[180,320]{1,0:T(8,128)} %get-tuple-element.28) | data formatting | bytes 460800
  (1 shorter events, 0.0 us)
Async XLA Ops:
  0.6 49.7 %copy-start = (bf16[2880,320]{0,1:T(8,128)(2,1)S(1)}, bf16[2880,320]{0,1:T(8,128)(2,1)}, u32[]{:S(2)}) copy-start(bf16[2880,320]{0,1:T(8,128)(2,1)} %param.10) | copy-start | bytes 5529604

commit v2 on v1

v2 whole, which is shorter than its diff:
```python
import jax
import jax.numpy as jnp
from jax import lax
from jax.experimental import pallas as pl
from jax.experimental.pallas import tpu as pltpu
from jax.sharding import PartitionSpec as P

F32 = jnp.float32
BF16 = jnp.bfloat16
GROUND_BIAS = 2.0
NF, NH, ND = 16, 8, 2
C = 320
CP = 384
HEADS = 5
T = 32
W = 16
ROWS = T * W
BLK = 128
NB = ROWS // BLK
NEG = -1e30
TOKENS = 2 * 32 * 128 * 16
GRAD_SCALE = float(TOKENS) ** -0.5
SCALING = 0.125


def peer(**where):
    return dict(device_id=where, device_id_type=pl.DeviceIdType.MESH)


def nn(a, b):
    return lax.dot_general(a, b, (((1,), (0,)), ((), ())), preferred_element_type=F32)


def nt(a, b):
    return lax.dot_general(a, b, (((1,), (1,)), ((), ())), preferred_element_type=F32)


def tn(a, b):
    return lax.dot_general(a, b, (((0,), (0,)), ((), ())), preferred_element_type=F32)


def pixel_major(src, tr, store, width):
    for s in range(0, width, 128):
        w = min(128, width - s)
        tr[s // 128, :, :w] = src[:, :, s : s + w].reshape(ROWS, w).astype(F32)
    for p in range(W):
        for s in range(0, width, 128):
            w = min(128, width - s)
            store(p, s, w, tr[s // 128, pl.ds(p, T, stride=W), :][:, :w].astype(BF16))


SLABS = ((0, 128, (0, 1)), (128, 128, (2, 3)), (256, 64, (4,)))


def block_kernel(
    x_ref, dy_ref, mark_ref, wat_ref, wct_ref, tb_ref,
    out_ref, attn_cr, conv_dr,
    xs, xt, dy0, dyu, dyd, wa, wc,
    tr, xp, dyp, q_s, k_s, v_s, o_s, pr, bias_s, y1_s, a_t, da_s, g_s, do_s, dq_s, dk_s, dv_s, x_t, o_t, cf,
    gi_s, attn_l, conv_l, conv_a, attn_a, conv_1, attn_1, conv_b, attn_b, conv_f, conv_c, conv_cr, conv_d, attn_c,
    xss, xsr, dss, dsr, hs, hr, gs, gr, pa, pb, cs, cr, as_, ar, c2s, c2r, c3s, c3r, a2s, a2r, lsem,
):
    f = lax.axis_index("frame")
    h = lax.axis_index("height")
    d = lax.axis_index("dp")
    other = 1 - d
    me = h * ND + d
    lin = h * NF + f
    prev = lax.rem(lin + NF * NH - 1, NF * NH)
    nxt = lax.rem(lin + 1, NF * NH)

    def remote(src, dst, ss, rs, **where):
        cp = pltpu.make_async_remote_copy(src_ref=src, dst_ref=dst, send_sem=ss, recv_sem=rs, **peer(**where))
        cp.start()
        return cp

    barrier = pltpu.get_barrier_semaphore()
    for k in range(1, NF):
        pl.semaphore_signal(barrier, inc=1, **peer(frame=lax.rem(f + k, NF)))
    for k in range(1, NH * ND):
        q = lax.rem(me + k, NH * ND)
        pl.semaphore_signal(barrier, inc=1, **peer(height=q // ND, dp=lax.rem(q, ND)))

    @pl.when(f == 0)
    def _():
        pl.semaphore_signal(barrier, inc=1, **peer(frame=lax.rem(prev, NF), height=prev // NF))

    @pl.when(f == NF - 1)
    def _():
        pl.semaphore_signal(barrier, inc=1, **peer(frame=lax.rem(nxt, NF), height=nxt // NF))

    lwa = pltpu.make_async_copy(wat_ref, wa, lsem.at[0])
    lwc = pltpu.make_async_copy(wct_ref, wc, lsem.at[1])
    lwa.start()
    lwc.start()

    xs[:, :, :, 0:256] = x_ref[:, :, :, 0:256]
    eye = lax.broadcasted_iota(jnp.int32, (1, W, W), 1) == lax.broadcasted_iota(jnp.int32, (1, W, W), 2)
    lane3 = lax.broadcasted_iota(jnp.int32, (1, W, 128), 2)
    for fr in range(2):
        mk = mark_ref[fr].astype(F32)
        col = jnp.sum(jnp.where(eye, mk[:, None, :], 0.0), axis=-1, keepdims=True)
        xs[fr, :, :, 256:384] = jnp.where(lane3 == 64, col, 0.0).astype(BF16)
    xs[:, :, :, 256:320] = x_ref[:, :, :, 256:320]

    edge = jnp.where(jnp.logical_or(f == 0, f == NF - 1), 1, 0)
    pl.semaphore_wait(barrier, NF + NH * ND - 2 + edge)

    xc, dc = [], []
    for k in range(1, NF):
        p = lax.rem(f + k, NF)
        xc.append(remote(xs.at[:, p], xt.at[pl.ds(2 * f, 2)], xss.at[k], xsr.at[k], frame=p))
    for k in range(1, NF):
        p = lax.rem(f + k, NF)
        dc.append(remote(dy_ref.at[:, p], dy0.at[pl.ds(2 * f, 2)], dss.at[k], dsr.at[k], frame=p))
    lx = pltpu.make_async_copy(xs.at[:, f], xt.at[pl.ds(2 * f, 2)], lsem.at[2])
    ld = pltpu.make_async_copy(dy_ref.at[:, f], dy0.at[pl.ds(2 * f, 2)], lsem.at[3])
    lx.start()
    ld.start()

    ri = lax.broadcasted_iota(jnp.int32, (BLK, BLK), 0) // T
    ci = lax.broadcasted_iota(jnp.int32, (BLK, BLK), 1) // T
    for hd in range(HEADS):
        one = tb_ref[hd]
        wide = jnp.concatenate([one] * 4, axis=1)
        full = jnp.concatenate([wide] * 4, axis=0)
        bias_s[hd] = jnp.where(ri == ci, full, NEG)
    zero = jnp.zeros((T, C), BF16)
    for r in range(3):
        dyp[r, 0:T, :] = zero
        dyp[r, (W + 1) * T :, :] = zero
    lane = lax.broadcasted_iota(jnp.int32, (BLK, 128), 1)
    low = lane < 64
    ones = jnp.full((8, 128), GROUND_BIAS, BF16)

    def only(val, i, w):
        if w == 64:
            return val
        keep = low if i == 0 else jnp.logical_not(low)
        return jnp.where(keep, val, jnp.zeros_like(val))

    def pick(parts, w):
        if w == 64:
            return parts[0]
        return jnp.where(low, parts[0], parts[1])

    lwa.wait()
    lx.wait()
    for cp in xc:
        cp.wait_recv()

    def put_x(p, s, w, val):
        xp[p * T : (p + 1) * T, s : s + w] = val

    pixel_major(xt, tr, put_x, CP)
    x = xp[:, :C]
    q_s[...] = nt(x, wa[:, 0:C]).astype(BF16)
    k_s[...] = nt(x, wa[:, C : 2 * C]).astype(BF16)
    v_s[...] = nt(x, wa[:, 2 * C : 3 * C]).astype(BF16)

    for b in range(NB):
        rows = slice(b * BLK, (b + 1) * BLK)
        marks = jnp.where(lane == 64, xp[rows, 256:384], jnp.zeros((BLK, 128), BF16))
        key_bias = nt(ones, marks)[0:1, :]
        for s, w, heads in SLABS:
            ls = slice(s, s + w)
            qb, kb, vb = q_s[rows, ls], k_s[rows, ls], v_s[rows, ls]
            outs = []
            for i, hd in enumerate(heads):
                sc = nt(only(qb, i, w), kb) * SCALING + bias_s[hd] + key_bias
                e = jnp.exp(sc - jnp.max(sc, axis=-1, keepdims=True))
                pf = e / jnp.sum(e, axis=-1, keepdims=True)
                pr[b, hd] = pf
                outs.append(nn(pf.astype(BF16), vb))
            o_s[rows, ls] = pick(outs, w).astype(BF16)

    ld.wait()
    for cp in dc:
        cp.wait_recv()
    up = remote(dy0, dyd, hs.at[0], hr.at[0], frame=lax.rem(prev, NF), height=prev // NF)
    down = remote(dy0, dyu, hs.at[1], hr.at[1], frame=lax.rem(nxt, NF), height=nxt // NF)

    y1 = (x.astype(F32) + nt(o_s[...], wa[:, 3 * C :])).astype(BF16)
    y1_s[...] = y1
    yf = y1.astype(F32)
    act = yf / (1.0 + jnp.exp(-yf))
    a_t[...] = act.T.astype(BF16)

    def place_row(r, src, keep):
        def put(p, s, w, val):
            if keep is not None:
                val = jnp.where(keep, val, jnp.zeros_like(val))
            dyp[r, (p + 1) * T : (p + 2) * T, s : s + w] = val

        pixel_major(src, tr, put, C)

    def tap_row(r, first):
        for c in range(3):
            tap = 3 * r + c
            off = (2 - c) * T
            shifted = dyp[r, off : off + ROWS, :]
            part = nn(shifted, wc[:, tap * C : (tap + 1) * C])
            da_s[...] = part if first else da_s[...] + part
            first = False
            cf[tap * C : (tap + 1) * C, :] = nn(a_t[...], shifted) * GRAD_SCALE

    lwc.wait()
    place_row(1, dy0, None)
    tap_row(1, True)
    x_t[...] = x.astype(F32).T.astype(BF16)
    o_t[...] = o_s[...].astype(F32).T.astype(BF16)
    up.wait_recv()
    place_row(0, dyd, lin < NF * NH - 1)
    tap_row(0, False)
    down.wait_recv()
    place_row(2, dyu, lin > 0)
    tap_row(2, False)

    for k in range(NH * ND):
        conv_l[k // ND, k % ND] = cf[k * 180 : (k + 1) * 180, :].astype(BF16)
    ca = remote(conv_l.at[:, other], conv_a, pa.at[0], pb.at[0], dp=other)

    yf = y1_s[...].astype(F32)
    sig = 1.0 / (1.0 + jnp.exp(-yf))
    slope = sig * (1.0 + yf * (1.0 - sig))
    g = (dyp[1, T : T + ROWS, :].astype(F32) + slope * da_s[...]).astype(BF16)
    g_s[...] = g
    do_s[...] = nn(g, wa[:, 3 * C :]).astype(BF16)

    ca.wait_recv()
    for j in range(NH):
        conv_1[j] = (conv_l[j, d].astype(F32) + conv_a[j].astype(F32)).astype(BF16)
    cc = []
    for k in range(1, NH):
        p = lax.rem(h + k, NH)
        cc.append(remote(conv_1.at[p], conv_b.at[k], cs.at[k], cr.at[k], height=p))

    for b in range(NB):
        rows = slice(b * BLK, (b + 1) * BLK)
        for s, w, heads in SLABS:
            ls = slice(s, s + w)
            qb, kb, vb, db = q_s[rows, ls], k_s[rows, ls], v_s[rows, ls], do_s[rows, ls]
            dqs, dks, dvs = [], [], []
            for i, hd in enumerate(heads):
                pf = pr[b, hd]
                dp = nt(only(db, i, w), vb)
                dsc = (pf * (dp - jnp.sum(pf * dp, axis=-1, keepdims=True))).astype(BF16)
                dqs.append(nn(dsc, kb))
                dks.append(tn(dsc, qb))
                dvs.append(tn(pf.astype(BF16), db))
            dq_s[rows, ls] = (pick(dqs, w) * SCALING).astype(BF16)
            dk_s[rows, ls] = (pick(dks, w) * SCALING).astype(BF16)
            dv_s[rows, ls] = pick(dvs, w).astype(BF16)

    dx = nn(dq_s[...], wa[:, 0:C]) + nn(dk_s[...], wa[:, C : 2 * C]) + nn(dv_s[...], wa[:, 2 * C : 3 * C])
    gi = g_s[...].astype(F32) + dx.astype(BF16).astype(F32)
    for s in range(0, C, 128):
        w = min(128, C - s)
        tr[s // 128, :, :w] = gi[:, s : s + w]
    for t in range(T):
        for s in range(0, C, 128):
            w = min(128, C - s)
            gi_s[t, :, s : s + w] = tr[s // 128, pl.ds(t, W, stride=T), :][:, :w].astype(BF16)
    gic = []
    for k in range(1, NF):
        p = lax.rem(f + k, NF)
        gic.append(remote(gi_s.at[pl.ds(2 * p, 2)], out_ref.at[:, f], gs.at[k], gr.at[k], frame=p))
    own = pltpu.make_async_copy(gi_s.at[pl.ds(2 * f, 2)], out_ref.at[:, f], lsem.at[4])
    own.start()

    for j, (left, right) in enumerate(((x_t, dq_s), (x_t, dk_s), (x_t, dv_s), (o_t, g_s))):
        term = nn(left[...], right[...]) * GRAD_SCALE
        for k in range(8):
            m = 8 * j + k
            attn_l[m // 2, m % 2] = term[40 * k : 40 * (k + 1), :].astype(BF16)
    aa = remote(attn_l.at[:, other], attn_a, pa.at[1], pb.at[1], dp=other)
    aa.wait_recv()
    for j in range(NF):
        attn_1[j] = (attn_l[j, d].astype(F32) + attn_a[j].astype(F32)).astype(BF16)
    ac = []
    for k in range(1, NF):
        p = lax.rem(f + k, NF)
        ac.append(remote(attn_1.at[p], attn_b.at[k], as_.at[k], ar.at[k], frame=p))

    total = conv_1[h].astype(F32)
    for k in range(1, NH):
        cc[k - 1].wait_recv()
        total = total + conv_b[k].astype(F32)
    conv_f[0:180, :] = total
    conv_f[180:192, :] = jnp.zeros((12, C), F32)
    for j in range(NF):
        conv_c[j] = conv_f[12 * j : 12 * j + 12, :].astype(BF16)
    c2 = []
    for k in range(1, NF):
        p = lax.rem(f + k, NF)
        c2.append(remote(conv_c.at[p], conv_cr.at[k], c2s.at[k], c2r.at[k], frame=p))

    total = attn_1[f].astype(F32)
    for k in range(1, NF):
        ac[k - 1].wait_recv()
        total = total + attn_b[k].astype(F32)
    for j in range(8):
        attn_c[j] = total[5 * j : 5 * j + 5, :]
    half = h // 4
    for j in range(8):
        th, td = 4 * d + j // 2, j % 2
        mine = jnp.logical_and(th == h, td == d)

        @pl.when(jnp.logical_not(mine))
        def _(j=j, th=th, td=td):
            remote(attn_c.at[j], attn_cr.at[h], a2s.at[j], a2r.at[h], height=th, dp=td)

        @pl.when(mine)
        def _(j=j):
            attn_cr[h] = attn_c[j]

    total = conv_c[f].astype(F32)
    for k in range(1, NF):
        c2[k - 1].wait_recv()
        total = total + conv_cr[k].astype(F32)
    conv_d[...] = total.astype(BF16)
    c3 = []
    for k in range(1, NF):
        p = lax.rem(f + k, NF)
        c3.append(remote(conv_d, conv_dr.at[f], c3s.at[k], c3r.at[k], frame=p))
    conv_dr[f] = total.astype(BF16)

    def arrived(i):
        return pltpu.make_async_remote_copy(
            src_ref=attn_c.at[0], dst_ref=attn_cr.at[i], send_sem=a2s.at[i], recv_sem=a2r.at[i], **peer(dp=other)
        )

    for i in range(8):
        @pl.when(jnp.logical_not(jnp.logical_and(i == h, d == half)))
        def _(i=i):
            arrived(i).wait_recv()

    own.wait()
    for cp in c3 + gic:
        cp.wait_recv()
    for cp in xc + dc + [up, down, ca, aa] + gic + cc + ac + c2 + c3:
        cp.wait_send()
    for j in range(8):
        th, td = 4 * d + j // 2, j % 2

        @pl.when(jnp.logical_not(jnp.logical_and(th == h, td == d)))
        def _(j=j):
            arrived(j).wait_send()


def block(x, dy, marks, wat, wct, tb):
    vm = pl.BlockSpec(memory_space=pltpu.VMEM)
    anyw = pl.BlockSpec(memory_space=pl.ANY)
    v = pltpu.VMEM
    dma = pltpu.SemaphoreType.DMA
    tok = v((ROWS, C), BF16)
    row = v((T, W, C), BF16)
    return pl.pallas_call(
        block_kernel,
        out_shape=(
            jax.ShapeDtypeStruct((2, W, W, C), BF16),
            jax.ShapeDtypeStruct((8, 5, C), F32),
            jax.ShapeDtypeStruct((NF, 12, C), BF16),
        ),
        in_specs=[vm, vm, vm, anyw, anyw, vm],
        out_specs=(vm, vm, vm),
        scratch_shapes=[
            v((2, W, W, CP), BF16), v((T, W, CP), BF16), row, row, row, v((C, 4 * C), BF16), v((C, 9 * C), BF16),
            v((3, ROWS, 128), F32), v((ROWS, CP), BF16), v((3, ROWS + 2 * T, C), BF16),
            tok, tok, tok, tok,
            v((NB, HEADS, BLK, BLK), F32), v((HEADS, BLK, BLK), F32),
            tok, v((C, ROWS), BF16), v((ROWS, C), F32), tok, tok, tok, tok, tok,
            v((C, ROWS), BF16), v((C, ROWS), BF16), v((9 * C, C), F32),
            row, v((NF, ND, 40, C), BF16), v((NH, ND, 180, C), BF16),
            v((NH, 180, C), BF16), v((NF, 40, C), BF16), v((NH, 180, C), BF16), v((NF, 40, C), BF16),
            v((NH, 180, C), BF16), v((NF, 40, C), BF16), v((192, C), F32), v((NF, 12, C), BF16), v((NF, 12, C), BF16),
            v((12, C), BF16), v((8, 5, C), F32),
            dma((NF,)), dma((NF,)), dma((NF,)), dma((NF,)), dma((2,)), dma((2,)),
            dma((NF,)), dma((NF,)), dma((2,)), dma((2,)), dma((NH,)), dma((NH,)), dma((NF,)), dma((NF,)),
            dma((NF,)), dma((NF,)), dma((NF,)), dma((NF,)), dma((8,)), dma((8,)), dma((5,)),
        ],
        compiler_params=pltpu.CompilerParams(collective_id=0, has_side_effects=True),
        name="block_backward",
    )(x, dy, marks, wat, wct, tb)


def finish_kernel(gi_ref, attn_ref, conv_ref, out_ref, oattn_ref, oconv_ref):
    out_ref[...] = gi_ref[...]
    total = attn_ref[0]
    for i in range(1, 8):
        total = total + attn_ref[i]
    oattn_ref[...] = total
    for j in range(NF - 1):
        oconv_ref[12 * j : 12 * j + 12, :] = conv_ref[j].astype(F32)


def finish(gi, attn, conv):
    vm = pl.BlockSpec(memory_space=pltpu.VMEM)
    return pl.pallas_call(
        finish_kernel,
        out_shape=(
            jax.ShapeDtypeStruct((2, W, W, C), BF16),
            jax.ShapeDtypeStruct((5, C), F32),
            jax.ShapeDtypeStruct((180, C), F32),
        ),
        in_specs=[vm] * 3,
        out_specs=(vm, vm, vm),
        name="finish",
    )(gi, attn, conv)


def body(clip_latents, out_grad, box_mask, attn_weights, conv_weights, time_bias):
    got = block(clip_latents[0], out_grad[0], box_mask[0], attn_weights.T, conv_weights.T, time_bias)
    out, oattn, oconv = finish(*got)
    return out[None], oattn, oconv


def solution(mesh):
    in_specs = (
        P("dp", "frame", "height", None, None),
        P("dp", "frame", "height", None, None),
        P("dp", "frame", "height", None),
        P(),
        P(),
        P(),
    )
    out_specs = (
        P("dp", "frame", "height", None, None),
        P(("frame", "height", "dp"), None),
        P(("height", "dp"), None),
    )
    return jax.shard_map(body, mesh=mesh, in_specs=in_specs, out_specs=out_specs, check_vma=False)
```

time: 132 us -> 95 us (0.72)
  Pallas kernels: 117 us -> 93.3 us
  local copies, waits for them, and re-layouts: 10 us -> 0 us
  other arithmetic: 2.71 us -> 0 us
    pallas_call x3 -> x2, Pallas kernels: 117 us -> 93.3 us  [the longest x1 91.3 us: block(): pl.pallas_call(block_kernel, out_shape=(jax.ShapeDtypeStruct((2, W, W, C)...]
    unnamed x7 -> x0, local copies, waits for them, and re-layouts: 9.65 us -> none
    concatenate x1 -> x0, other arithmetic: 1.87 us -> none  [body(): jnp.concatenate([x, marks, jnp.zeros(x.shape[:3] + (CP - C - 1,), BF16)],...]
where the time goes in v2:
time: 95 us; the launch traced here: 93.9 us
  Pallas kernels  93.3 us (98%)
    pallas_call x1, Pallas kernels, block(): pl.pallas_call(block_kernel, out_shape=(jax.ShapeDtypeStruct((2, W, W, C)...  91.3 us
    pallas_call x1, Pallas kernels, finish(): pl.pallas_call(finish_kernel, out_shape=(jax.ShapeDtypeStruct((2, W, W, C...  1.98 us

profile of v2, /device:TPU:2, one launch (start us, length us, event | category | flops | bytes accessed | tf_op | source)
XLA Modules:
  0.0 93.9 jit_solution(10485059397942461716)
XLA Ops:
  0.6 91.3 %block_backward.1 = (bf16[2,16,16,320]{3,2,1,0:T(8,128)(2,1)}, f32[8,5,320]{2,1,0:T(8,128)}, bf16[16,12,320]{2,1,0:T(8,128)(2,1)}) custom-call(bf16[2,16,16,320]{3,2,1,0:T(8,128)(2,1)} %bitcast.8, bf16[2,16,16,320]{3,2,1,0:T(8,128)(2,1)} %bitcast.9, s32[2,16,16]{2,1,0:T(8,128)} %bitcast.10, bf16[320,1280]{1,0:T(8,128)(2,1)} %bitcast.7, ...), custom_call_target="tpu_custom_call" | custom-call | tf_op jit(solution)/shard_map/block_backward/pallas_call | solution.py:358
  91.9 2.0 %finish.1 = (bf16[2,16,16,320]{3,2,1,0:T(8,128)(2,1)}, f32[5,320]{1,0:T(8,128)}, f32[180,320]{1,0:T(8,128)}) custom-call(bf16[2,16,16,320]{3,2,1,0:T(8,128)(2,1)} %get-tuple-element.9.gi_ref, f32[8,5,320]{2,1,0:T(8,128)} %get-tuple-element.10.attn_ref, bf16[16,12,320]{2,1,0:T(8,128)(2,1)} %get-tuple-element.11.conv_ref), custom_call_target="tpu_custom_call" | custom-call | tf_op jit(solution)/shard_map/finish/pallas_call | solution.py:399

commit v3 on v2

--- a/solution.py
+++ b/solution.py
@@ -49,6 +49,7 @@
             store(p, s, w, tr[s // 128, pl.ds(p, T, stride=W), :][:, :w].astype(BF16))
 
 
+ORDER = (1, 15, 8, 2, 14, 7, 9, 3, 13, 6, 10, 4, 12, 5, 11)
 SLABS = ((0, 128, (0, 1)), (128, 128, (2, 3)), (256, 64, (4,)))
 
 
@@ -57,7 +58,7 @@
     out_ref, attn_cr, conv_dr,
     xs, xt, dy0, dyu, dyd, wa, wc,
     tr, xp, dyp, q_s, k_s, v_s, o_s, pr, bias_s, y1_s, a_t, da_s, g_s, do_s, dq_s, dk_s, dv_s, x_t, o_t, cf,
-    gi_s, attn_l, conv_l, conv_a, attn_a, conv_1, attn_1, conv_b, attn_b, conv_f, conv_c, conv_cr, conv_d, attn_c,
+    gi_s, attn_f, attn_l, conv_l, conv_a, attn_a, conv_1, attn_1, conv_b, attn_b, conv_f, conv_c, conv_cr, conv_d, attn_g, attn_c,
     xss, xsr, dss, dsr, hs, hr, gs, gr, pa, pb, cs, cr, as_, ar, c2s, c2r, c3s, c3r, a2s, a2r, lsem,
 ):
     f = lax.axis_index("frame")
@@ -117,6 +118,23 @@
     ld = pltpu.make_async_copy(dy_ref.at[:, f], dy0.at[pl.ds(2 * f, 2)], lsem.at[3])
     lx.start()
     ld.start()
+    fwd = []
+
+    def forward(k):
+        part = pl.ds(2 * lax.rem(f + NF - k, NF), 2)
+        up = remote(dy0.at[part], dyd.at[part], hs.at[0, k], hr.at[0, k], frame=lax.rem(prev, NF), height=prev // NF)
+        down = remote(dy0.at[part], dyu.at[part], hs.at[1, k], hr.at[1, k], frame=lax.rem(nxt, NF), height=nxt // NF)
+        fwd.append((up, down))
+
+    ld.wait()
+    forward(0)
+    waiting = list(ORDER)
+
+    def forward_next():
+        if waiting:
+            k = waiting.pop(0)
+            dc[k - 1].wait_recv()
+            forward(k)
 
     ri = lax.broadcasted_iota(jnp.int32, (BLK, BLK), 0) // T
     ci = lax.broadcasted_iota(jnp.int32, (BLK, BLK), 1) // T
@@ -146,8 +164,8 @@
 
     lwa.wait()
     lx.wait()
-    for cp in xc:
-        cp.wait_recv()
+    for k in ORDER:
+        xc[k - 1].wait_recv()
 
     def put_x(p, s, w, val):
         xp[p * T : (p + 1) * T, s : s + w] = val
@@ -173,12 +191,9 @@
                 pr[b, hd] = pf
                 outs.append(nn(pf.astype(BF16), vb))
             o_s[rows, ls] = pick(outs, w).astype(BF16)
-
-    ld.wait()
-    for cp in dc:
-        cp.wait_recv()
-    up = remote(dy0, dyd, hs.at[0], hr.at[0], frame=lax.rem(prev, NF), height=prev // NF)
-    down = remote(dy0, dyu, hs.at[1], hr.at[1], frame=lax.rem(nxt, NF), height=nxt // NF)
+            forward_next()
+    while waiting:
+        forward_next()
 
     y1 = (x.astype(F32) + nt(o_s[...], wa[:, 3 * C :])).astype(BF16)
     y1_s[...] = y1
@@ -207,12 +222,20 @@
     lwc.wait()
     place_row(1, dy0, None)
     tap_row(1, True)
-    x_t[...] = x.astype(F32).T.astype(BF16)
-    o_t[...] = o_s[...].astype(F32).T.astype(BF16)
-    up.wait_recv()
+    rr = lax.broadcasted_iota(jnp.int32, (C, C), 0)
+    cc_ = lax.broadcasted_iota(jnp.int32, (C, C), 1)
+    mm = (rr * 3277) >> 16
+    rem = rr - 20 * mm
+    cf_ = (rem * 13108) >> 16
+    perm = jnp.where(cc_ == 80 * cf_ + 5 * mm + (rem - 5 * cf_), 1.0, 0.0).astype(BF16)
+    x_t[...] = nt(perm, x).astype(BF16)
+    o_t[...] = nt(perm, o_s[...]).astype(BF16)
+    for up, _ in fwd:
+        up.wait_recv()
     place_row(0, dyd, lin < NF * NH - 1)
     tap_row(0, False)
-    down.wait_recv()
+    for _, down in fwd:
+        down.wait_recv()
     place_row(2, dyu, lin > 0)
     tap_row(2, False)
 
@@ -270,17 +293,18 @@
 
     for j, (left, right) in enumerate(((x_t, dq_s), (x_t, dk_s), (x_t, dv_s), (o_t, g_s))):
         term = nn(left[...], right[...]) * GRAD_SCALE
-        for k in range(8):
-            m = 8 * j + k
-            attn_l[m // 2, m % 2] = term[40 * k : 40 * (k + 1), :].astype(BF16)
+        for m in range(NH * ND):
+            attn_f[m, 20 * j : 20 * j + 20, :] = term[20 * m : 20 * m + 20, :]
+    for m in range(NH * ND):
+        attn_l[m // ND, m % ND] = attn_f[m].astype(BF16)
     aa = remote(attn_l.at[:, other], attn_a, pa.at[1], pb.at[1], dp=other)
     aa.wait_recv()
-    for j in range(NF):
+    for j in range(NH):
         attn_1[j] = (attn_l[j, d].astype(F32) + attn_a[j].astype(F32)).astype(BF16)
     ac = []
-    for k in range(1, NF):
-        p = lax.rem(f + k, NF)
-        ac.append(remote(attn_1.at[p], attn_b.at[k], as_.at[k], ar.at[k], frame=p))
+    for k in range(1, NH):
+        p = lax.rem(h + k, NH)
+        ac.append(remote(attn_1.at[p], attn_b.at[k], as_.at[k], ar.at[k], height=p))
 
     total = conv_1[h].astype(F32)
     for k in range(1, NH):
@@ -295,24 +319,18 @@
         p = lax.rem(f + k, NF)
         c2.append(remote(conv_c.at[p], conv_cr.at[k], c2s.at[k], c2r.at[k], frame=p))
 
-    total = attn_1[f].astype(F32)
-    for k in range(1, NF):
+    total = attn_1[h].astype(F32)
+    for k in range(1, NH):
         ac[k - 1].wait_recv()
         total = total + attn_b[k].astype(F32)
-    for j in range(8):
-        attn_c[j] = total[5 * j : 5 * j + 5, :]
-    half = h // 4
-    for j in range(8):
-        th, td = 4 * d + j // 2, j % 2
-        mine = jnp.logical_and(th == h, td == d)
-
-        @pl.when(jnp.logical_not(mine))
-        def _(j=j, th=th, td=td):
-            remote(attn_c.at[j], attn_cr.at[h], a2s.at[j], a2r.at[h], height=th, dp=td)
-
-        @pl.when(mine)
-        def _(j=j):
-            attn_cr[h] = attn_c[j]
+    attn_g[...] = total
+    for j in range(NF):
+        attn_c[j] = attn_g[5 * j : 5 * j + 5, :]
+    a2 = []
+    for k in range(1, NF):
+        p = lax.rem(f + k, NF)
+        a2.append(remote(attn_c.at[p], attn_cr.at[k], a2s.at[k], a2r.at[k], frame=p))
+    attn_cr[0] = attn_c[f]
 
     total = conv_c[f].astype(F32)
     for k in range(1, NF):
@@ -325,27 +343,14 @@
         c3.append(remote(conv_d, conv_dr.at[f], c3s.at[k], c3r.at[k], frame=p))
     conv_dr[f] = total.astype(BF16)
 
-    def arrived(i):
-        return pltpu.make_async_remote_copy(
-            src_ref=attn_c.at[0], dst_ref=attn_cr.at[i], send_sem=a2s.at[i], recv_sem=a2r.at[i], **peer(dp=other)
-        )
-
-    for i in range(8):
-        @pl.when(jnp.logical_not(jnp.logical_and(i == h, d == half)))
-        def _(i=i):
-            arrived(i).wait_recv()
-
     own.wait()
-    for cp in c3 + gic:
+    for cp in a2 + c3 + gic:
         cp.wait_recv()
-    for cp in xc + dc + [up, down, ca, aa] + gic + cc + ac + c2 + c3:
+    for cp in xc + dc + [ca, aa] + gic + cc + ac + a2 + c2 + c3:
         cp.wait_send()
-    for j in range(8):
-        th, td = 4 * d + j // 2, j % 2
-
-        @pl.when(jnp.logical_not(jnp.logical_and(th == h, td == d)))
-        def _(j=j):
-            arrived(j).wait_send()
+    for up, down in fwd:
+        up.wait_send()
+        down.wait_send()
 
 
 def block(x, dy, marks, wat, wct, tb):
@@ -359,7 +364,7 @@
         block_kernel,
         out_shape=(
             jax.ShapeDtypeStruct((2, W, W, C), BF16),
-            jax.ShapeDtypeStruct((8, 5, C), F32),
+            jax.ShapeDtypeStruct((NF, 5, C), F32),
             jax.ShapeDtypeStruct((NF, 12, C), BF16),
         ),
         in_specs=[vm, vm, vm, anyw, anyw, vm],
@@ -371,13 +376,13 @@
             v((NB, HEADS, BLK, BLK), F32), v((HEADS, BLK, BLK), F32),
             tok, v((C, ROWS), BF16), v((ROWS, C), F32), tok, tok, tok, tok, tok,
             v((C, ROWS), BF16), v((C, ROWS), BF16), v((9 * C, C), F32),
-            row, v((NF, ND, 40, C), BF16), v((NH, ND, 180, C), BF16),
-            v((NH, 180, C), BF16), v((NF, 40, C), BF16), v((NH, 180, C), BF16), v((NF, 40, C), BF16),
-            v((NH, 180, C), BF16), v((NF, 40, C), BF16), v((192, C), F32), v((NF, 12, C), BF16), v((NF, 12, C), BF16),
-            v((12, C), BF16), v((8, 5, C), F32),
-            dma((NF,)), dma((NF,)), dma((NF,)), dma((NF,)), dma((2,)), dma((2,)),
-            dma((NF,)), dma((NF,)), dma((2,)), dma((2,)), dma((NH,)), dma((NH,)), dma((NF,)), dma((NF,)),
-            dma((NF,)), dma((NF,)), dma((NF,)), dma((NF,)), dma((8,)), dma((8,)), dma((5,)),
+            row, v((NH * ND, 80, C), F32), v((NH, ND, 80, C), BF16), v((NH, ND, 180, C), BF16),
+            v((NH, 180, C), BF16), v((NH, 80, C), BF16), v((NH, 180, C), BF16), v((NH, 80, C), BF16),
+            v((NH, 180, C), BF16), v((NH, 80, C), BF16), v((192, C), F32), v((NF, 12, C), BF16), v((NF, 12, C), BF16),
+            v((12, C), BF16), v((80, C), F32), v((NF, 5, C), F32),
+            dma((NF,)), dma((NF,)), dma((NF,)), dma((NF,)), dma((2, NF)), dma((2, NF)),
+            dma((NF,)), dma((NF,)), dma((2,)), dma((2,)), dma((NH,)), dma((NH,)), dma((NH,)), dma((NH,)),
+            dma((NF,)), dma((NF,)), dma((NF,)), dma((NF,)), dma((NF,)), dma((NF,)), dma((5,)),
         ],
         compiler_params=pltpu.CompilerParams(collective_id=0, has_side_effects=True),
         name="block_backward",
@@ -387,7 +392,7 @@
 def finish_kernel(gi_ref, attn_ref, conv_ref, out_ref, oattn_ref, oconv_ref):
     out_ref[...] = gi_ref[...]
     total = attn_ref[0]
-    for i in range(1, 8):
+    for i in range(1, NF):
         total = total + attn_ref[i]
     oattn_ref[...] = total
     for j in range(NF - 1):

time: 95 us -> 90.6 us (0.954)
  the two profiles are of different devices: /device:TPU:2 before, /device:TPU:25 now
where the time goes in v3:
time: 90.6 us
  Pallas kernels  89.9 us (99%)
    pallas_call x1, Pallas kernels, block(): pl.pallas_call(block_kernel, out_shape=(jax.ShapeDtypeStruct((2, W, W, C)...  87.9 us
    pallas_call x1, Pallas kernels, finish(): pl.pallas_call(finish_kernel, out_shape=(jax.ShapeDtypeStruct((2, W, W, C...  2.05 us

profile of v3, /device:TPU:25, one launch (start us, length us, event | category | flops | bytes accessed | tf_op | source)
XLA Modules:
  0.0 90.6 jit_solution(627408682342862763)
XLA Ops:
  0.6 87.9 %block_backward.1 = (bf16[2,16,16,320]{3,2,1,0:T(8,128)(2,1)}, f32[16,5,320]{2,1,0:T(8,128)}, bf16[16,12,320]{2,1,0:T(8,128)(2,1)}) custom-call(bf16[2,16,16,320]{3,2,1,0:T(8,128)(2,1)} %bitcast.8, bf16[2,16,16,320]{3,2,1,0:T(8,128)(2,1)} %bitcast.9, s32[2,16,16]{2,1,0:T(8,128)} %bitcast.10, bf16[320,1280]{1,0:T(8,128)(2,1)} %bitcast.7, ...), custom_call_target="tpu_custom_call" | custom-call | tf_op jit(solution)/shard_map/block_backward/pallas_call | solution.py:363
  88.5 2.0 %finish.1 = (bf16[2,16,16,320]{3,2,1,0:T(8,128)(2,1)}, f32[5,320]{1,0:T(8,128)}, f32[180,320]{1,0:T(8,128)}) custom-call(bf16[2,16,16,320]{3,2,1,0:T(8,128)(2,1)} %get-tuple-element.9.gi_ref, f32[16,5,320]{2,1,0:T(8,128)} %get-tuple-element.10.attn_ref, bf16[16,12,320]{2,1,0:T(8,128)(2,1)} %get-tuple-element.11.conv_ref), custom_call_target="tpu_custom_call" | custom-call | tf_op jit(solution)/shard_map/finish/pallas_call | solution.py:404

commit v4 on v3

--- a/solution.py
+++ b/solution.py
@@ -10,7 +10,7 @@
 GROUND_BIAS = 2.0
 NF, NH, ND = 16, 8, 2
 C = 320
-CP = 384
+PK = 640
 HEADS = 5
 T = 32
 W = 16
@@ -39,14 +39,20 @@
     return lax.dot_general(a, b, (((0,), (0,)), ((), ())), preferred_element_type=F32)
 
 
-def pixel_major(src, tr, store, width):
-    for s in range(0, width, 128):
-        w = min(128, width - s)
-        tr[s // 128, :, :w] = src[:, :, s : s + w].reshape(ROWS, w).astype(F32)
+def pixel_major(src, tr, store):
+    for s in range(5):
+        tr[s, 0 : NF * W, :] = src[:, :, 128 * s : 128 * s + 128].reshape(NF * W, 128).astype(F32)
     for p in range(W):
-        for s in range(0, width, 128):
-            w = min(128, width - s)
-            store(p, s, w, tr[s // 128, pl.ds(p, T, stride=W), :][:, :w].astype(BF16))
+        for e in range(2):
+            for s in range(2):
+                store(p, e, 128 * s, 128, tr[2 * e + s, pl.ds(p, NF, stride=W), :].astype(BF16))
+            store(p, e, 256, 64, tr[4, pl.ds(p, NF, stride=W), :][:, 64 * e : 64 * e + 64].astype(BF16))
+
+
+def pack(src, dst):
+    for e in range(2):
+        dst[:, :, 256 * e : 256 * e + 256] = src[e, :, :, 0:256]
+    dst[:, :, 512:640] = jnp.concatenate([src[0, :, :, 256:320], src[1, :, :, 256:320]], axis=-1)
 
 
 ORDER = (1, 15, 8, 2, 14, 7, 9, 3, 13, 6, 10, 4, 12, 5, 11)
@@ -56,10 +62,10 @@
 def block_kernel(
     x_ref, dy_ref, mark_ref, wat_ref, wct_ref, tb_ref,
     out_ref, attn_cr, conv_dr,
-    xs, xt, dy0, dyu, dyd, wa, wc,
+    xs, ys, ms, mt, xt, dy0, dyu, dyd, wa, wc,
     tr, xp, dyp, q_s, k_s, v_s, o_s, pr, bias_s, y1_s, a_t, da_s, g_s, do_s, dq_s, dk_s, dv_s, x_t, o_t, cf,
     gi_s, attn_f, attn_l, conv_l, conv_a, attn_a, conv_1, attn_1, conv_b, attn_b, conv_f, conv_c, conv_cr, conv_d, attn_g, attn_c,
-    xss, xsr, dss, dsr, hs, hr, gs, gr, pa, pb, cs, cr, as_, ar, c2s, c2r, c3s, c3r, a2s, a2r, lsem,
+    mss, msr, xss, xsr, dss, dsr, hs, hr, gs, gr, pa, pb, cs, cr, as_, ar, c2s, c2r, c3s, c3r, a2s, a2r, lsem,
 ):
     f = lax.axis_index("frame")
     h = lax.axis_index("height")
@@ -95,33 +101,32 @@
     lwa.start()
     lwc.start()
 
-    xs[:, :, :, 0:256] = x_ref[:, :, :, 0:256]
-    eye = lax.broadcasted_iota(jnp.int32, (1, W, W), 1) == lax.broadcasted_iota(jnp.int32, (1, W, W), 2)
-    lane3 = lax.broadcasted_iota(jnp.int32, (1, W, 128), 2)
-    for fr in range(2):
-        mk = mark_ref[fr].astype(F32)
-        col = jnp.sum(jnp.where(eye, mk[:, None, :], 0.0), axis=-1, keepdims=True)
-        xs[fr, :, :, 256:384] = jnp.where(lane3 == 64, col, 0.0).astype(BF16)
-    xs[:, :, :, 256:320] = x_ref[:, :, :, 256:320]
+    pack(x_ref, xs)
+    ms[:, 0, :] = jnp.zeros((NF, 128), F32)
+    ms[:, 0, 0 : 2 * W] = jnp.concatenate([mark_ref[0], mark_ref[1]], axis=-1).astype(F32)
+    pack(dy_ref, ys)
 
     edge = jnp.where(jnp.logical_or(f == 0, f == NF - 1), 1, 0)
     pl.semaphore_wait(barrier, NF + NH * ND - 2 + edge)
 
-    xc, dc = [], []
-    for k in range(1, NF):
-        p = lax.rem(f + k, NF)
-        xc.append(remote(xs.at[:, p], xt.at[pl.ds(2 * f, 2)], xss.at[k], xsr.at[k], frame=p))
-    for k in range(1, NF):
-        p = lax.rem(f + k, NF)
-        dc.append(remote(dy_ref.at[:, p], dy0.at[pl.ds(2 * f, 2)], dss.at[k], dsr.at[k], frame=p))
-    lx = pltpu.make_async_copy(xs.at[:, f], xt.at[pl.ds(2 * f, 2)], lsem.at[2])
-    ld = pltpu.make_async_copy(dy_ref.at[:, f], dy0.at[pl.ds(2 * f, 2)], lsem.at[3])
+    xc, mc, dc = [], [], []
+    for k in range(1, NF):
+        p = lax.rem(f + k, NF)
+        mc.append(remote(ms.at[p], mt.at[f], mss.at[k], msr.at[k], frame=p))
+        xc.append(remote(xs.at[p], xt.at[f], xss.at[k], xsr.at[k], frame=p))
+    for k in range(1, NF):
+        p = lax.rem(f + k, NF)
+        dc.append(remote(ys.at[p], dy0.at[f], dss.at[k], dsr.at[k], frame=p))
+    lx = pltpu.make_async_copy(xs.at[f], xt.at[f], lsem.at[2])
+    ld = pltpu.make_async_copy(ys.at[f], dy0.at[f], lsem.at[3])
+    lm = pltpu.make_async_copy(ms.at[f], mt.at[f], lsem.at[5])
     lx.start()
     ld.start()
+    lm.start()
     fwd = []
 
     def forward(k):
-        part = pl.ds(2 * lax.rem(f + NF - k, NF), 2)
+        part = lax.rem(f + NF - k, NF)
         up = remote(dy0.at[part], dyd.at[part], hs.at[0, k], hr.at[0, k], frame=lax.rem(prev, NF), height=prev // NF)
         down = remote(dy0.at[part], dyu.at[part], hs.at[1, k], hr.at[1, k], frame=lax.rem(nxt, NF), height=nxt // NF)
         fwd.append((up, down))
@@ -138,8 +143,17 @@
 
     ri = lax.broadcasted_iota(jnp.int32, (BLK, BLK), 0) // T
     ci = lax.broadcasted_iota(jnp.int32, (BLK, BLK), 1) // T
+    tq = lax.broadcasted_iota(jnp.int32, (T, T), 0)
+    tu = lax.broadcasted_iota(jnp.int32, (T, T), 1)
+    turn = jnp.where(tu == 2 * (tq & (NF - 1)) + (tq >> 4), 1.0, 0.0)
+
+    def exact(left, right, dim):
+        return lax.dot_general(
+            left, right, (((1,), (dim,)), ((), ())), precision=lax.Precision.HIGHEST, preferred_element_type=F32
+        )
+
     for hd in range(HEADS):
-        one = tb_ref[hd]
+        one = exact(exact(turn, tb_ref[hd], 0), turn, 1)
         wide = jnp.concatenate([one] * 4, axis=1)
         full = jnp.concatenate([wide] * 4, axis=0)
         bias_s[hd] = jnp.where(ri == ci, full, NEG)
@@ -164,21 +178,26 @@
 
     lwa.wait()
     lx.wait()
+    lm.wait()
     for k in ORDER:
+        mc[k - 1].wait_recv()
         xc[k - 1].wait_recv()
 
-    def put_x(p, s, w, val):
-        xp[p * T : (p + 1) * T, s : s + w] = val
-
-    pixel_major(xt, tr, put_x, CP)
-    x = xp[:, :C]
+    def put_x(p, e, s, w, val):
+        xp[p * T + e * NF : p * T + (e + 1) * NF, s : s + w] = val
+
+    pixel_major(xt, tr, put_x)
+    x = xp[...]
+    marks_all = jnp.concatenate([mt[:, 0, :]] * 8, axis=0)
+    row_b = lax.broadcasted_iota(jnp.int32, (BLK, 128), 0)
+    home = ((row_b >> 4) & 1) * W + (row_b >> 5)
     q_s[...] = nt(x, wa[:, 0:C]).astype(BF16)
     k_s[...] = nt(x, wa[:, C : 2 * C]).astype(BF16)
     v_s[...] = nt(x, wa[:, 2 * C : 3 * C]).astype(BF16)
 
     for b in range(NB):
         rows = slice(b * BLK, (b + 1) * BLK)
-        marks = jnp.where(lane == 64, xp[rows, 256:384], jnp.zeros((BLK, 128), BF16))
+        marks = jnp.where(lane == home + 4 * b, marks_all, 0.0).astype(BF16)
         key_bias = nt(ones, marks)[0:1, :]
         for s, w, heads in SLABS:
             ls = slice(s, s + w)
@@ -202,12 +221,13 @@
     a_t[...] = act.T.astype(BF16)
 
     def place_row(r, src, keep):
-        def put(p, s, w, val):
+        def put(p, e, s, w, val):
             if keep is not None:
                 val = jnp.where(keep, val, jnp.zeros_like(val))
-            dyp[r, (p + 1) * T : (p + 2) * T, s : s + w] = val
-
-        pixel_major(src, tr, put, C)
+            at = (p + 1) * T + e * NF
+            dyp[r, at : at + NF, s : s + w] = val
+
+        pixel_major(src, tr, put)
 
     def tap_row(r, first):
         for c in range(3):
@@ -250,6 +270,12 @@
     g_s[...] = g
     do_s[...] = nn(g, wa[:, 3 * C :]).astype(BF16)
 
+    def attn_term(j, left, right):
+        term = nn(left[...], right[...]) * GRAD_SCALE
+        for m in range(NH * ND):
+            attn_f[m, 20 * j : 20 * j + 20, :] = term[20 * m : 20 * m + 20, :]
+
+    attn_term(3, o_t, g_s)
     ca.wait_recv()
     for j in range(NH):
         conv_1[j] = (conv_l[j, d].astype(F32) + conv_a[j].astype(F32)).astype(BF16)
@@ -275,29 +301,31 @@
             dk_s[rows, ls] = (pick(dks, w) * SCALING).astype(BF16)
             dv_s[rows, ls] = pick(dvs, w).astype(BF16)
 
-    dx = nn(dq_s[...], wa[:, 0:C]) + nn(dk_s[...], wa[:, C : 2 * C]) + nn(dv_s[...], wa[:, 2 * C : 3 * C])
-    gi = g_s[...].astype(F32) + dx.astype(BF16).astype(F32)
-    for s in range(0, C, 128):
-        w = min(128, C - s)
-        tr[s // 128, :, :w] = gi[:, s : s + w]
-    for t in range(T):
-        for s in range(0, C, 128):
-            w = min(128, C - s)
-            gi_s[t, :, s : s + w] = tr[s // 128, pl.ds(t, W, stride=T), :][:, :w].astype(BF16)
-    gic = []
-    for k in range(1, NF):
-        p = lax.rem(f + k, NF)
-        gic.append(remote(gi_s.at[pl.ds(2 * p, 2)], out_ref.at[:, f], gs.at[k], gr.at[k], frame=p))
-    own = pltpu.make_async_copy(gi_s.at[pl.ds(2 * f, 2)], out_ref.at[:, f], lsem.at[4])
-    own.start()
-
-    for j, (left, right) in enumerate(((x_t, dq_s), (x_t, dk_s), (x_t, dv_s), (o_t, g_s))):
-        term = nn(left[...], right[...]) * GRAD_SCALE
-        for m in range(NH * ND):
-            attn_f[m, 20 * j : 20 * j + 20, :] = term[20 * m : 20 * m + 20, :]
+    for j, right in enumerate((dq_s, dk_s, dv_s)):
+        attn_term(j, x_t, right)
     for m in range(NH * ND):
         attn_l[m // ND, m % ND] = attn_f[m].astype(BF16)
     aa = remote(attn_l.at[:, other], attn_a, pa.at[1], pb.at[1], dp=other)
+
+    dx = nn(dq_s[...], wa[:, 0:C]) + nn(dk_s[...], wa[:, C : 2 * C]) + nn(dv_s[...], wa[:, 2 * C : 3 * C])
+    gi = g_s[...].astype(F32) + dx.astype(BF16).astype(F32)
+    for s in range(2):
+        tr[s] = gi[:, 128 * s : 128 * s + 128]
+    tr[2, :, 0:64] = gi[:, 256:320]
+    for t in range(NF):
+        for e in range(2):
+            for s in range(2):
+                at = 256 * e + 128 * s
+                gi_s[t, :, at : at + 128] = tr[s, pl.ds(e * NF + t, W, stride=T), :].astype(BF16)
+        ends = [tr[2, pl.ds(e * NF + t, W, stride=T), :][:, 0:64] for e in range(2)]
+        gi_s[t, :, 512:640] = jnp.concatenate(ends, axis=-1).astype(BF16)
+    gic = []
+    for k in range(1, NF):
+        p = lax.rem(f + k, NF)
+        gic.append(remote(gi_s.at[p], out_ref.at[f], gs.at[k], gr.at[k], frame=p))
+    own = pltpu.make_async_copy(gi_s.at[f], out_ref.at[f], lsem.at[4])
+    own.start()
+
     aa.wait_recv()
     for j in range(NH):
         attn_1[j] = (attn_l[j, d].astype(F32) + attn_a[j].astype(F32)).astype(BF16)
@@ -346,7 +374,7 @@
     own.wait()
     for cp in a2 + c3 + gic:
         cp.wait_recv()
-    for cp in xc + dc + [ca, aa] + gic + cc + ac + a2 + c2 + c3:
+    for cp in mc + xc + dc + [ca, aa] + gic + cc + ac + a2 + c2 + c3:
         cp.wait_send()
     for up, down in fwd:
         up.wait_send()
@@ -359,19 +387,20 @@
     v = pltpu.VMEM
     dma = pltpu.SemaphoreType.DMA
     tok = v((ROWS, C), BF16)
-    row = v((T, W, C), BF16)
+    row = v((NF, W, PK), BF16)
+    mark = v((NF, 1, 128), F32)
     return pl.pallas_call(
         block_kernel,
         out_shape=(
-            jax.ShapeDtypeStruct((2, W, W, C), BF16),
+            jax.ShapeDtypeStruct((W, W, PK), BF16),
             jax.ShapeDtypeStruct((NF, 5, C), F32),
             jax.ShapeDtypeStruct((NF, 12, C), BF16),
         ),
         in_specs=[vm, vm, vm, anyw, anyw, vm],
         out_specs=(vm, vm, vm),
         scratch_shapes=[
-            v((2, W, W, CP), BF16), v((T, W, CP), BF16), row, row, row, v((C, 4 * C), BF16), v((C, 9 * C), BF16),
-            v((3, ROWS, 128), F32), v((ROWS, CP), BF16), v((3, ROWS + 2 * T, C), BF16),
+            row, row, mark, mark, row, row, row, row, v((C, 4 * C), BF16), v((C, 9 * C), BF16),
+            v((5, ROWS, 128), F32), v((ROWS, C), BF16), v((3, ROWS + 2 * T, C), BF16),
             tok, tok, tok, tok,
             v((NB, HEADS, BLK, BLK), F32), v((HEADS, BLK, BLK), F32),
             tok, v((C, ROWS), BF16), v((ROWS, C), F32), tok, tok, tok, tok, tok,
@@ -380,9 +409,9 @@
             v((NH, 180, C), BF16), v((NH, 80, C), BF16), v((NH, 180, C), BF16), v((NH, 80, C), BF16),
             v((NH, 180, C), BF16), v((NH, 80, C), BF16), v((192, C), F32), v((NF, 12, C), BF16), v((NF, 12, C), BF16),
             v((12, C), BF16), v((80, C), F32), v((NF, 5, C), F32),
-            dma((NF,)), dma((NF,)), dma((NF,)), dma((NF,)), dma((2, NF)), dma((2, NF)),
+            dma((NF,)), dma((NF,)), dma((NF,)), dma((NF,)), dma((NF,)), dma((NF,)), dma((2, NF)), dma((2, NF)),
             dma((NF,)), dma((NF,)), dma((2,)), dma((2,)), dma((NH,)), dma((NH,)), dma((NH,)), dma((NH,)),
-            dma((NF,)), dma((NF,)), dma((NF,)), dma((NF,)), dma((NF,)), dma((NF,)), dma((5,)),
+            dma((NF,)), dma((NF,)), dma((NF,)), dma((NF,)), dma((NF,)), dma((NF,)), dma((6,)),
         ],
         compiler_params=pltpu.CompilerParams(collective_id=0, has_side_effects=True),
         name="block_backward",
@@ -390,7 +419,9 @@
 
 
 def finish_kernel(gi_ref, attn_ref, conv_ref, out_ref, oattn_ref, oconv_ref):
-    out_ref[...] = gi_ref[...]
+    for e in range(2):
+        out_ref[e, :, :, 0:256] = gi_ref[:, :, 256 * e : 256 * e + 256]
+        out_ref[e, :, :, 256:320] = gi_ref[:, :, 512 + 64 * e : 576 + 64 * e]
     total = attn_ref[0]
     for i in range(1, NF):
         total = total + attn_ref[i]

time: 90.6 us -> 87.5 us (0.966)
  Pallas kernels: 89.9 us -> 86.7 us
    pallas_call x1, Pallas kernels: 87.9 us -> 84.7 us  [block(): pl.pallas_call(block_kernel, out_shape=(jax.ShapeDtypeStruct((W, W, PK),...]
where the time goes in v4:
time: 87.5 us; the launch traced here: 87.3 us
  Pallas kernels  86.7 us (99%)
    pallas_call x1, Pallas kernels, block(): pl.pallas_call(block_kernel, out_shape=(jax.ShapeDtypeStruct((W, W, PK),...  84.7 us
    pallas_call x1, Pallas kernels, finish(): pl.pallas_call(finish_kernel, out_shape=(jax.ShapeDtypeStruct((2, W, W, C...  2.03 us

profile of v4, /device:TPU:25, one launch (start us, length us, event | category | flops | bytes accessed | tf_op | source)
XLA Modules:
  0.0 87.3 jit_solution(6379091476719484841)
XLA Ops:
  0.6 84.7 %block_backward.1 = (bf16[16,16,640]{2,1,0:T(8,128)(2,1)}, f32[16,5,320]{2,1,0:T(8,128)}, bf16[16,12,320]{2,1,0:T(8,128)(2,1)}) custom-call(bf16[2,16,16,320]{3,2,1,0:T(8,128)(2,1)} %bitcast.8, bf16[2,16,16,320]{3,2,1,0:T(8,128)(2,1)} %bitcast.9, s32[2,16,16]{2,1,0:T(8,128)} %bitcast.10, bf16[320,1280]{1,0:T(8,128)(2,1)} %bitcast.7, ...), custom_call_target="tpu_custom_call" | custom-call | tf_op jit(solution)/shard_map/block_backward/pallas_call | solution.py:392
  85.3 2.0 %finish.1 = (bf16[2,16,16,320]{3,2,1,0:T(8,128)(2,1)}, f32[5,320]{1,0:T(8,128)}, f32[180,320]{1,0:T(8,128)}) custom-call(bf16[16,16,640]{2,1,0:T(8,128)(2,1)} %get-tuple-element.9.gi_ref, f32[16,5,320]{2,1,0:T(8,128)} %get-tuple-element.10.attn_ref, bf16[16,12,320]{2,1,0:T(8,128)(2,1)} %get-tuple-element.11.conv_ref), custom_call_target="tpu_custom_call" | custom-call | tf_op jit(solution)/shard_map/finish/pallas_call | solution.py:435

commit v5 on v4

--- a/solution.py
+++ b/solution.py
@@ -64,7 +64,7 @@
     out_ref, attn_cr, conv_dr,
     xs, ys, ms, mt, xt, dy0, dyu, dyd, wa, wc,
     tr, xp, dyp, q_s, k_s, v_s, o_s, pr, bias_s, y1_s, a_t, da_s, g_s, do_s, dq_s, dk_s, dv_s, x_t, o_t, cf,
-    gi_s, attn_f, attn_l, conv_l, conv_a, attn_a, conv_1, attn_1, conv_b, attn_b, conv_f, conv_c, conv_cr, conv_d, attn_g, attn_c,
+    gi_s, attn_f, attn_l, conv_l, conv_a, attn_a, conv_1, attn_1, conv_b, attn_b, conv_f, conv_c, conv_cr, conv_d, attn_g, attn_w, attn_c,
     mss, msr, xss, xsr, dss, dsr, hs, hr, gs, gr, pa, pb, cs, cr, as_, ar, c2s, c2r, c3s, c3r, a2s, a2r, lsem,
 ):
     f = lax.axis_index("frame")
@@ -157,6 +157,9 @@
         wide = jnp.concatenate([one] * 4, axis=1)
         full = jnp.concatenate([wide] * 4, axis=0)
         bias_s[hd] = jnp.where(ri == ci, full, NEG)
+    conv_l[...] = jnp.zeros_like(conv_l)
+    attn_f[...] = jnp.zeros_like(attn_f)
+    attn_w[...] = jnp.zeros_like(attn_w)
     zero = jnp.zeros((T, C), BF16)
     for r in range(3):
         dyp[r, 0:T, :] = zero
@@ -254,14 +257,48 @@
         up.wait_recv()
     place_row(0, dyd, lin < NF * NH - 1)
     tap_row(0, False)
+
+    def halve(first, last, i):
+        for k in range(ND * first, ND * last):
+            at = 180 * k
+            to = conv_l.at[k // ND, k % ND]
+            to[0:180, :] = cf[at : at + 180, 0:128].astype(BF16)
+            to[192:372, :] = cf[at : at + 180, 128:256].astype(BF16)
+            ends = [cf[at : at + 90, 256:320], cf[at + 90 : at + 180, 256:320]]
+            to[384:474, :] = jnp.concatenate(ends, axis=-1).astype(BF16)
+        part = pl.ds(first, last - first)
+        return remote(conv_l.at[part, other], conv_a.at[part], pa.at[i], pb.at[i], dp=other)
+
+    cc = []
+    for k in range(1, NH):
+        cc.append(
+            pltpu.make_async_remote_copy(
+                src_ref=conv_1.at[lax.rem(h + k, NH)],
+                dst_ref=conv_b.at[k],
+                send_sem=cs.at[k],
+                recv_sem=cr.at[k],
+                **peer(height=lax.rem(h + k, NH)),
+            )
+        )
+
+    def spread(first, last):
+        for j in range(first, last):
+            conv_1[j] = (conv_l[j, d].astype(F32) + conv_a[j].astype(F32)).astype(BF16)
+        for k in range(1, NH):
+            p = lax.rem(h + k, NH)
+
+            @pl.when(jnp.logical_and(p >= first, p < last))
+            def _(k=k):
+                cc[k - 1].start()
+
+    ca = halve(0, 5, 0)
     for _, down in fwd:
         down.wait_recv()
     place_row(2, dyu, lin > 0)
     tap_row(2, False)
-
-    for k in range(NH * ND):
-        conv_l[k // ND, k % ND] = cf[k * 180 : (k + 1) * 180, :].astype(BF16)
-    ca = remote(conv_l.at[:, other], conv_a, pa.at[0], pb.at[0], dp=other)
+    cb = halve(5, NH, 2)
+    ca.wait_recv()
+    spread(0, 5)
 
     yf = y1_s[...].astype(F32)
     sig = 1.0 / (1.0 + jnp.exp(-yf))
@@ -273,16 +310,14 @@
     def attn_term(j, left, right):
         term = nn(left[...], right[...]) * GRAD_SCALE
         for m in range(NH * ND):
-            attn_f[m, 20 * j : 20 * j + 20, :] = term[20 * m : 20 * m + 20, :]
-
+            piece = term[20 * m : 20 * m + 20, :]
+            attn_f[m, 20 * j : 20 * j + 20, :] = piece[:, 0:128]
+            attn_f[m, 80 + 20 * j : 100 + 20 * j, :] = piece[:, 128:256]
+            attn_f[m, 160 + 10 * j : 170 + 10 * j, :] = jnp.concatenate([piece[0:10, 256:], piece[10:20, 256:]], axis=-1)
+
+    cb.wait_recv()
+    spread(5, NH)
     attn_term(3, o_t, g_s)
-    ca.wait_recv()
-    for j in range(NH):
-        conv_1[j] = (conv_l[j, d].astype(F32) + conv_a[j].astype(F32)).astype(BF16)
-    cc = []
-    for k in range(1, NH):
-        p = lax.rem(h + k, NH)
-        cc.append(remote(conv_1.at[p], conv_b.at[k], cs.at[k], cr.at[k], height=p))
 
     for b in range(NB):
         rows = slice(b * BLK, (b + 1) * BLK)
@@ -338,10 +373,10 @@
     for k in range(1, NH):
         cc[k - 1].wait_recv()
         total = total + conv_b[k].astype(F32)
-    conv_f[0:180, :] = total
-    conv_f[180:192, :] = jnp.zeros((12, C), F32)
+    conv_f[0:480, :] = total
+    conv_f[480:512, :] = jnp.zeros((32, 128), F32)
     for j in range(NF):
-        conv_c[j] = conv_f[12 * j : 12 * j + 12, :].astype(BF16)
+        conv_c[j] = conv_f[32 * j : 32 * j + 32, :].astype(BF16)
     c2 = []
     for k in range(1, NF):
         p = lax.rem(f + k, NF)
@@ -353,7 +388,13 @@
         total = total + attn_b[k].astype(F32)
     attn_g[...] = total
     for j in range(NF):
-        attn_c[j] = attn_g[5 * j : 5 * j + 5, :]
+        at = 160 + 10 * (j // 4) + 5 * (j % 2)
+        to = 64 * (j % 4 // 2)
+        attn_w[j, 0:5, :] = attn_g[5 * j : 5 * j + 5, :]
+        attn_w[j, 5:10, :] = attn_g[80 + 5 * j : 85 + 5 * j, :]
+        attn_w[j, 10:15, 0:64] = attn_g[at : at + 5, to : to + 64]
+    for j in range(NF):
+        attn_c[j] = attn_w[j].astype(BF16)
     a2 = []
     for k in range(1, NF):
         p = lax.rem(f + k, NF)
@@ -374,7 +415,7 @@
     own.wait()
     for cp in a2 + c3 + gic:
         cp.wait_recv()
-    for cp in mc + xc + dc + [ca, aa] + gic + cc + ac + a2 + c2 + c3:
+    for cp in mc + xc + dc + [ca, cb, aa] + gic + cc + ac + a2 + c2 + c3:
         cp.wait_send()
     for up, down in fwd:
         up.wait_send()
@@ -393,8 +434,8 @@
         block_kernel,
         out_shape=(
             jax.ShapeDtypeStruct((W, W, PK), BF16),
-            jax.ShapeDtypeStruct((NF, 5, C), F32),
-            jax.ShapeDtypeStruct((NF, 12, C), BF16),
+            jax.ShapeDtypeStruct((NF, 16, 128), BF16),
+            jax.ShapeDtypeStruct((NF, 32, 128), BF16),
         ),
         in_specs=[vm, vm, vm, anyw, anyw, vm],
         out_specs=(vm, vm, vm),
@@ -405,12 +446,13 @@
             v((NB, HEADS, BLK, BLK), F32), v((HEADS, BLK, BLK), F32),
             tok, v((C, ROWS), BF16), v((ROWS, C), F32), tok, tok, tok, tok, tok,
             v((C, ROWS), BF16), v((C, ROWS), BF16), v((9 * C, C), F32),
-            row, v((NH * ND, 80, C), F32), v((NH, ND, 80, C), BF16), v((NH, ND, 180, C), BF16),
-            v((NH, 180, C), BF16), v((NH, 80, C), BF16), v((NH, 180, C), BF16), v((NH, 80, C), BF16),
-            v((NH, 180, C), BF16), v((NH, 80, C), BF16), v((192, C), F32), v((NF, 12, C), BF16), v((NF, 12, C), BF16),
-            v((12, C), BF16), v((80, C), F32), v((NF, 5, C), F32),
+            row, v((NH * ND, 208, 128), F32), v((NH, ND, 208, 128), BF16), v((NH, ND, 480, 128), BF16),
+            v((NH, 480, 128), BF16), v((NH, 208, 128), BF16), v((NH, 480, 128), BF16), v((NH, 208, 128), BF16),
+            v((NH, 480, 128), BF16), v((NH, 208, 128), BF16),
+            v((512, 128), F32), v((NF, 32, 128), BF16), v((NF, 32, 128), BF16), v((32, 128), BF16),
+            v((208, 128), F32), v((NF, 16, 128), F32), v((NF, 16, 128), BF16),
             dma((NF,)), dma((NF,)), dma((NF,)), dma((NF,)), dma((NF,)), dma((NF,)), dma((2, NF)), dma((2, NF)),
-            dma((NF,)), dma((NF,)), dma((2,)), dma((2,)), dma((NH,)), dma((NH,)), dma((NH,)), dma((NH,)),
+            dma((NF,)), dma((NF,)), dma((3,)), dma((3,)), dma((NH,)), dma((NH,)), dma((NH,)), dma((NH,)),
             dma((NF,)), dma((NF,)), dma((NF,)), dma((NF,)), dma((NF,)), dma((NF,)), dma((6,)),
         ],
         compiler_params=pltpu.CompilerParams(collective_id=0, has_side_effects=True),
@@ -422,12 +464,17 @@
     for e in range(2):
         out_ref[e, :, :, 0:256] = gi_ref[:, :, 256 * e : 256 * e + 256]
         out_ref[e, :, :, 256:320] = gi_ref[:, :, 512 + 64 * e : 576 + 64 * e]
-    total = attn_ref[0]
+    total = attn_ref[0].astype(F32)
     for i in range(1, NF):
-        total = total + attn_ref[i]
-    oattn_ref[...] = total
-    for j in range(NF - 1):
-        oconv_ref[12 * j : 12 * j + 12, :] = conv_ref[j].astype(F32)
+        total = total + attn_ref[i].astype(F32)
+    oattn_ref[:, 0:128] = total[0:5]
+    oattn_ref[:, 128:256] = total[5:10]
+    oattn_ref[:, 256:320] = total[10:15, 0:64]
+    conv = conv_ref[...].astype(F32).reshape(32 * NF, 128)
+    oconv_ref[:, 0:128] = conv[0:180]
+    oconv_ref[:, 128:256] = conv[192:372]
+    oconv_ref[0:90, 256:320] = conv[384:474, 0:64]
+    oconv_ref[90:180, 256:320] = conv[384:474, 64:128]
 
 
 def finish(gi, attn, conv):

time: 87.5 us -> 81 us (0.926)
  the two profiles are of different devices: /device:TPU:25 before, /device:TPU:2 now
where the time goes in v5:
time: 81 us; the launch traced here: 80.8 us
  Pallas kernels  80.2 us (99%)
    pallas_call x1, Pallas kernels, block(): pl.pallas_call(block_kernel, out_shape=(jax.ShapeDtypeStruct((W, W, PK),...  78.2 us
    pallas_call x1, Pallas kernels, finish(): pl.pallas_call(finish_kernel, out_shape=(jax.ShapeDtypeStruct((2, W, W, C...  1.98 us

profile of v5, /device:TPU:2, one launch (start us, length us, event | category | flops | bytes accessed | tf_op | source)
XLA Modules:
  0.0 80.8 jit_solution(16582836004512352143)
XLA Ops:
  0.6 78.2 %block_backward.1 = (bf16[16,16,640]{2,1,0:T(8,128)(2,1)}, bf16[16,16,128]{2,1,0:T(8,128)(2,1)}, bf16[16,32,128]{2,1,0:T(8,128)(2,1)}) custom-call(bf16[2,16,16,320]{3,2,1,0:T(8,128)(2,1)} %bitcast.8, bf16[2,16,16,320]{3,2,1,0:T(8,128)(2,1)} %bitcast.9, s32[2,16,16]{2,1,0:T(8,128)} %bitcast.10, bf16[320,1280]{1,0:T(8,128)(2,1)} %bitcast.7, ...), custom_call_target="tpu_custom_call" | custom-call | tf_op jit(solution)/shard_map/block_backward/pallas_call | solution.py:433
  78.8 2.0 %finish.1 = (bf16[2,16,16,320]{3,2,1,0:T(8,128)(2,1)}, f32[5,320]{1,0:T(8,128)}, f32[180,320]{1,0:T(8,128)}) custom-call(bf16[16,16,640]{2,1,0:T(8,128)(2,1)} %get-tuple-element.9.gi_ref, bf16[16,16,128]{2,1,0:T(8,128)(2,1)} %get-tuple-element.10.attn_ref, bf16[16,32,128]{2,1,0:T(8,128)(2,1)} %get-tuple-element.11.conv_ref), custom_call_target="tpu_custom_call" | custom-call | tf_op jit(solution)/shard_map/finish/pallas_call | solution.py:482

commit v6 on v5

--- a/solution.py
+++ b/solution.py
@@ -60,9 +60,9 @@
 
 
 def block_kernel(
-    x_ref, dy_ref, mark_ref, wat_ref, wct_ref, tb_ref,
+    x_hbm, dy_hbm, mark_ref, wat_ref, wct_ref, tb_ref,
     out_ref, attn_cr, conv_dr,
-    xs, ys, ms, mt, xt, dy0, dyu, dyd, wa, wc,
+    x_ref, dy_ref, xs, ys, ms, mt, xt, dy0, dyu, dyd, wa, wc,
     tr, xp, dyp, q_s, k_s, v_s, o_s, pr, bias_s, y1_s, a_t, da_s, g_s, do_s, dq_s, dk_s, dv_s, x_t, o_t, cf,
     gi_s, attn_f, attn_l, conv_l, conv_a, attn_a, conv_1, attn_1, conv_b, attn_b, conv_f, conv_c, conv_cr, conv_d, attn_g, attn_w, attn_c,
     mss, msr, xss, xsr, dss, dsr, hs, hr, gs, gr, pa, pb, cs, cr, as_, ar, c2s, c2r, c3s, c3r, a2s, a2r, lsem,
@@ -81,6 +81,10 @@
         cp.start()
         return cp
 
+    inx = pltpu.make_async_copy(x_hbm, x_ref, lsem.at[6])
+    iny = pltpu.make_async_copy(dy_hbm, dy_ref, lsem.at[7])
+    inx.start()
+    iny.start()
     barrier = pltpu.get_barrier_semaphore()
     for k in range(1, NF):
         pl.semaphore_signal(barrier, inc=1, **peer(frame=lax.rem(f + k, NF)))
@@ -101,9 +105,11 @@
     lwa.start()
     lwc.start()
 
+    inx.wait()
     pack(x_ref, xs)
     ms[:, 0, :] = jnp.zeros((NF, 128), F32)
     ms[:, 0, 0 : 2 * W] = jnp.concatenate([mark_ref[0], mark_ref[1]], axis=-1).astype(F32)
+    iny.wait()
     pack(dy_ref, ys)
 
     edge = jnp.where(jnp.logical_or(f == 0, f == NF - 1), 1, 0)
@@ -232,19 +238,61 @@
 
         pixel_major(src, tr, put)
 
-    def tap_row(r, first):
+    def shifted(c, r):
+        return dyp[r, (2 - c) * T : (2 - c) * T + ROWS, :]
+
+    def kernel_taps(r):
         for c in range(3):
             tap = 3 * r + c
-            off = (2 - c) * T
-            shifted = dyp[r, off : off + ROWS, :]
-            part = nn(shifted, wc[:, tap * C : (tap + 1) * C])
+            cf[tap * C : (tap + 1) * C, :] = nn(a_t[...], shifted(c, r)) * GRAD_SCALE
+
+    def data_taps(r, first):
+        for c in range(3):
+            tap = 3 * r + c
+            part = nn(shifted(c, r), wc[:, tap * C : (tap + 1) * C])
             da_s[...] = part if first else da_s[...] + part
             first = False
-            cf[tap * C : (tap + 1) * C, :] = nn(a_t[...], shifted) * GRAD_SCALE
-
+
+    def halve(first, last, i):
+        for k in range(ND * first, ND * last):
+            at = 180 * k
+            to = conv_l.at[k // ND, k % ND]
+            to[0:180, :] = cf[at : at + 180, 0:128].astype(BF16)
+            to[192:372, :] = cf[at : at + 180, 128:256].astype(BF16)
+            ends = [cf[at : at + 90, 256:320], cf[at + 90 : at + 180, 256:320]]
+            to[384:474, :] = jnp.concatenate(ends, axis=-1).astype(BF16)
+        part = pl.ds(first, last - first)
+        return remote(conv_l.at[part, other], conv_a.at[part], pa.at[i], pb.at[i], dp=other)
+
+    cc = []
+    for k in range(1, NH):
+        cc.append(
+            pltpu.make_async_remote_copy(
+                src_ref=conv_1.at[lax.rem(h + k, NH)],
+                dst_ref=conv_b.at[k],
+                send_sem=cs.at[k],
+                recv_sem=cr.at[k],
+                **peer(height=lax.rem(h + k, NH)),
+            )
+        )
+
+    def spread(first, last):
+        for j in range(first, last):
+            conv_1[j] = (conv_l[j, d].astype(F32) + conv_a[j].astype(F32)).astype(BF16)
+        for k in range(1, NH):
+            p = lax.rem(h + k, NH)
+
+            @pl.when(jnp.logical_and(p >= first, p < last))
+            def _(k=k):
+                cc[k - 1].start()
+
+    place_row(1, dy0, None)
+    kernel_taps(1)
+    ca = halve(3, 5, 0)
     lwc.wait()
-    place_row(1, dy0, None)
-    tap_row(1, True)
+    data_taps(1, True)
+    ca.wait_recv()
+    spread(3, 5)
     rr = lax.broadcasted_iota(jnp.int32, (C, C), 0)
     cc_ = lax.broadcasted_iota(jnp.int32, (C, C), 1)
     mm = (rr * 3277) >> 16
@@ -256,49 +304,19 @@
     for up, _ in fwd:
         up.wait_recv()
     place_row(0, dyd, lin < NF * NH - 1)
-    tap_row(0, False)
-
-    def halve(first, last, i):
-        for k in range(ND * first, ND * last):
-            at = 180 * k
-            to = conv_l.at[k // ND, k % ND]
-            to[0:180, :] = cf[at : at + 180, 0:128].astype(BF16)
-            to[192:372, :] = cf[at : at + 180, 128:256].astype(BF16)
-            ends = [cf[at : at + 90, 256:320], cf[at + 90 : at + 180, 256:320]]
-            to[384:474, :] = jnp.concatenate(ends, axis=-1).astype(BF16)
-        part = pl.ds(first, last - first)
-        return remote(conv_l.at[part, other], conv_a.at[part], pa.at[i], pb.at[i], dp=other)
-
-    cc = []
-    for k in range(1, NH):
-        cc.append(
-            pltpu.make_async_remote_copy(
-                src_ref=conv_1.at[lax.rem(h + k, NH)],
-                dst_ref=conv_b.at[k],
-                send_sem=cs.at[k],
-                recv_sem=cr.at[k],
-                **peer(height=lax.rem(h + k, NH)),
-            )
-        )
-
-    def spread(first, last):
-        for j in range(first, last):
-            conv_1[j] = (conv_l[j, d].astype(F32) + conv_a[j].astype(F32)).astype(BF16)
-        for k in range(1, NH):
-            p = lax.rem(h + k, NH)
-
-            @pl.when(jnp.logical_and(p >= first, p < last))
-            def _(k=k):
-                cc[k - 1].start()
-
-    ca = halve(0, 5, 0)
+    kernel_taps(0)
+    cb = halve(0, 3, 2)
     for _, down in fwd:
         down.wait_recv()
     place_row(2, dyu, lin > 0)
-    tap_row(2, False)
-    cb = halve(5, NH, 2)
-    ca.wait_recv()
-    spread(0, 5)
+    kernel_taps(2)
+    cd = halve(5, NH, 3)
+    data_taps(0, False)
+    cb.wait_recv()
+    spread(0, 3)
+    data_taps(2, False)
+    cd.wait_recv()
+    spread(5, NH)
 
     yf = y1_s[...].astype(F32)
     sig = 1.0 / (1.0 + jnp.exp(-yf))
@@ -315,8 +333,6 @@
             attn_f[m, 80 + 20 * j : 100 + 20 * j, :] = piece[:, 128:256]
             attn_f[m, 160 + 10 * j : 170 + 10 * j, :] = jnp.concatenate([piece[0:10, 256:], piece[10:20, 256:]], axis=-1)
 
-    cb.wait_recv()
-    spread(5, NH)
     attn_term(3, o_t, g_s)
 
     for b in range(NB):
@@ -342,6 +358,19 @@
         attn_l[m // ND, m % ND] = attn_f[m].astype(BF16)
     aa = remote(attn_l.at[:, other], attn_a, pa.at[1], pb.at[1], dp=other)
 
+    total = conv_1[h].astype(F32)
+    for k in range(1, NH):
+        cc[k - 1].wait_recv()
+        total = total + conv_b[k].astype(F32)
+    conv_f[0:480, :] = total
+    conv_f[480:512, :] = jnp.zeros((32, 128), F32)
+    for j in range(NF):
+        conv_c[j] = conv_f[32 * j : 32 * j + 32, :].astype(BF16)
+    c2 = []
+    for k in range(1, NF):
+        p = lax.rem(f + k, NF)
+        c2.append(remote(conv_c.at[p], conv_cr.at[k], c2s.at[k], c2r.at[k], frame=p))
+
     dx = nn(dq_s[...], wa[:, 0:C]) + nn(dk_s[...], wa[:, C : 2 * C]) + nn(dv_s[...], wa[:, 2 * C : 3 * C])
     gi = g_s[...].astype(F32) + dx.astype(BF16).astype(F32)
     for s in range(2):
@@ -368,19 +397,6 @@
     for k in range(1, NH):
         p = lax.rem(h + k, NH)
         ac.append(remote(attn_1.at[p], attn_b.at[k], as_.at[k], ar.at[k], height=p))
-
-    total = conv_1[h].astype(F32)
-    for k in range(1, NH):
-        cc[k - 1].wait_recv()
-        total = total + conv_b[k].astype(F32)
-    conv_f[0:480, :] = total
-    conv_f[480:512, :] = jnp.zeros((32, 128), F32)
-    for j in range(NF):
-        conv_c[j] = conv_f[32 * j : 32 * j + 32, :].astype(BF16)
-    c2 = []
-    for k in range(1, NF):
-        p = lax.rem(f + k, NF)
-        c2.append(remote(conv_c.at[p], conv_cr.at[k], c2s.at[k], c2r.at[k], frame=p))
 
     total = attn_1[h].astype(F32)
     for k in range(1, NH):
@@ -415,7 +431,7 @@
     own.wait()
     for cp in a2 + c3 + gic:
         cp.wait_recv()
-    for cp in mc + xc + dc + [ca, cb, aa] + gic + cc + ac + a2 + c2 + c3:
+    for cp in mc + xc + dc + [ca, cb, cd, aa] + gic + cc + ac + a2 + c2 + c3:
         cp.wait_send()
     for up, down in fwd:
         up.wait_send()
@@ -437,10 +453,10 @@
             jax.ShapeDtypeStruct((NF, 16, 128), BF16),
             jax.ShapeDtypeStruct((NF, 32, 128), BF16),
         ),
-        in_specs=[vm, vm, vm, anyw, anyw, vm],
+        in_specs=[anyw, anyw, vm, anyw, anyw, vm],
         out_specs=(vm, vm, vm),
         scratch_shapes=[
-            row, row, mark, mark, row, row, row, row, v((C, 4 * C), BF16), v((C, 9 * C), BF16),
+            v((2, W, W, C), BF16), v((2, W, W, C), BF16), row, row, mark, mark, row, row, row, row, v((C, 4 * C), BF16), v((C, 9 * C), BF16),
             v((5, ROWS, 128), F32), v((ROWS, C), BF16), v((3, ROWS + 2 * T, C), BF16),
             tok, tok, tok, tok,
             v((NB, HEADS, BLK, BLK), F32), v((HEADS, BLK, BLK), F32),
@@ -452,8 +468,8 @@
             v((512, 128), F32), v((NF, 32, 128), BF16), v((NF, 32, 128), BF16), v((32, 128), BF16),
             v((208, 128), F32), v((NF, 16, 128), F32), v((NF, 16, 128), BF16),
             dma((NF,)), dma((NF,)), dma((NF,)), dma((NF,)), dma((NF,)), dma((NF,)), dma((2, NF)), dma((2, NF)),
-            dma((NF,)), dma((NF,)), dma((3,)), dma((3,)), dma((NH,)), dma((NH,)), dma((NH,)), dma((NH,)),
-            dma((NF,)), dma((NF,)), dma((NF,)), dma((NF,)), dma((NF,)), dma((NF,)), dma((6,)),
+            dma((NF,)), dma((NF,)), dma((4,)), dma((4,)), dma((NH,)), dma((NH,)), dma((NH,)), dma((NH,)),
+            dma((NF,)), dma((NF,)), dma((NF,)), dma((NF,)), dma((NF,)), dma((NF,)), dma((8,)),
         ],
         compiler_params=pltpu.CompilerParams(collective_id=0, has_side_effects=True),
         name="block_backward",

time: 81 us -> 81.8 us (level)
  the two profiles are of different devices: /device:TPU:2 before, /device:TPU:26 now
where the time goes in v6:
time: 81.8 us; the launch traced here: 81.7 us
  Pallas kernels  81 us (99%)
    pallas_call x1, Pallas kernels, block(): pl.pallas_call(block_kernel, out_shape=(jax.ShapeDtypeStruct((W, W, PK),...  79 us
    pallas_call x1, Pallas kernels, finish(): pl.pallas_call(finish_kernel, out_shape=(jax.ShapeDtypeStruct((2, W, W, C...  1.98 us

profile of v6, /device:TPU:26, one launch (start us, length us, event | category | flops | bytes accessed | tf_op | source)
XLA Modules:
  0.0 81.7 jit_solution(11446800067495799704)
XLA Ops:
  0.6 79.0 %block_backward.1 = (bf16[16,16,640]{2,1,0:T(8,128)(2,1)}, bf16[16,16,128]{2,1,0:T(8,128)(2,1)}, bf16[16,32,128]{2,1,0:T(8,128)(2,1)}) custom-call(bf16[2,16,16,320]{3,2,1,0:T(8,128)(2,1)} %bitcast.8, bf16[2,16,16,320]{3,2,1,0:T(8,128)(2,1)} %bitcast.9, s32[2,16,16]{2,1,0:T(8,128)} %bitcast.10, bf16[320,1280]{1,0:T(8,128)(2,1)} %bitcast.7, ...), custom_call_target="tpu_custom_call" | custom-call | tf_op jit(solution)/shard_map/block_backward/pallas_call | solution.py:449
  79.7 2.0 %finish.1 = (bf16[2,16,16,320]{3,2,1,0:T(8,128)(2,1)}, f32[5,320]{1,0:T(8,128)}, f32[180,320]{1,0:T(8,128)}) custom-call(bf16[16,16,640]{2,1,0:T(8,128)(2,1)} %get-tuple-element.9.gi_ref, bf16[16,16,128]{2,1,0:T(8,128)(2,1)} %get-tuple-element.10.attn_ref, bf16[16,32,128]{2,1,0:T(8,128)(2,1)} %get-tuple-element.11.conv_ref), custom_call_target="tpu_custom_call" | custom-call | tf_op jit(solution)/shard_map/finish/pallas_call | solution.py:498

commit v7 on v6

--- a/solution.py
+++ b/solution.py
@@ -352,25 +352,6 @@
             dk_s[rows, ls] = (pick(dks, w) * SCALING).astype(BF16)
             dv_s[rows, ls] = pick(dvs, w).astype(BF16)
 
-    for j, right in enumerate((dq_s, dk_s, dv_s)):
-        attn_term(j, x_t, right)
-    for m in range(NH * ND):
-        attn_l[m // ND, m % ND] = attn_f[m].astype(BF16)
-    aa = remote(attn_l.at[:, other], attn_a, pa.at[1], pb.at[1], dp=other)
-
-    total = conv_1[h].astype(F32)
-    for k in range(1, NH):
-        cc[k - 1].wait_recv()
-        total = total + conv_b[k].astype(F32)
-    conv_f[0:480, :] = total
-    conv_f[480:512, :] = jnp.zeros((32, 128), F32)
-    for j in range(NF):
-        conv_c[j] = conv_f[32 * j : 32 * j + 32, :].astype(BF16)
-    c2 = []
-    for k in range(1, NF):
-        p = lax.rem(f + k, NF)
-        c2.append(remote(conv_c.at[p], conv_cr.at[k], c2s.at[k], c2r.at[k], frame=p))
-
     dx = nn(dq_s[...], wa[:, 0:C]) + nn(dk_s[...], wa[:, C : 2 * C]) + nn(dv_s[...], wa[:, 2 * C : 3 * C])
     gi = g_s[...].astype(F32) + dx.astype(BF16).astype(F32)
     for s in range(2):
@@ -389,6 +370,25 @@
         gic.append(remote(gi_s.at[p], out_ref.at[f], gs.at[k], gr.at[k], frame=p))
     own = pltpu.make_async_copy(gi_s.at[f], out_ref.at[f], lsem.at[4])
     own.start()
+
+    for j, right in enumerate((dq_s, dk_s, dv_s)):
+        attn_term(j, x_t, right)
+    for m in range(NH * ND):
+        attn_l[m // ND, m % ND] = attn_f[m].astype(BF16)
+    aa = remote(attn_l.at[:, other], attn_a, pa.at[1], pb.at[1], dp=other)
+
+    total = conv_1[h].astype(F32)
+    for k in range(1, NH):
+        cc[k - 1].wait_recv()
+        total = total + conv_b[k].astype(F32)
+    conv_f[0:480, :] = total
+    conv_f[480:512, :] = jnp.zeros((32, 128), F32)
+    for j in range(NF):
+        conv_c[j] = conv_f[32 * j : 32 * j + 32, :].astype(BF16)
+    c2 = []
+    for k in range(1, NF):
+        p = lax.rem(f + k, NF)
+        c2.append(remote(conv_c.at[p], conv_cr.at[k], c2s.at[k], c2r.at[k], frame=p))
 
     aa.wait_recv()
     for j in range(NH):

time: 81.8 us -> 79.9 us (0.977)
  the two profiles are of different devices: /device:TPU:26 before, /device:TPU:2 now
where the time goes in v7:
time: 79.9 us; the launch traced here: 79.7 us
  Pallas kernels  79 us (99%)
    pallas_call x1, Pallas kernels, block(): pl.pallas_call(block_kernel, out_shape=(jax.ShapeDtypeStruct((W, W, PK),...  77.1 us
    pallas_call x1, Pallas kernels, finish(): pl.pallas_call(finish_kernel, out_shape=(jax.ShapeDtypeStruct((2, W, W, C...  1.98 us

profile of v7, /device:TPU:2, one launch (start us, length us, event | category | flops | bytes accessed | tf_op | source)
XLA Modules:
  0.0 79.7 jit_solution(7408691854944331566)
XLA Ops:
  0.6 77.1 %block_backward.1 = (bf16[16,16,640]{2,1,0:T(8,128)(2,1)}, bf16[16,16,128]{2,1,0:T(8,128)(2,1)}, bf16[16,32,128]{2,1,0:T(8,128)(2,1)}) custom-call(bf16[2,16,16,320]{3,2,1,0:T(8,128)(2,1)} %bitcast.8, bf16[2,16,16,320]{3,2,1,0:T(8,128)(2,1)} %bitcast.9, s32[2,16,16]{2,1,0:T(8,128)} %bitcast.10, bf16[320,1280]{1,0:T(8,128)(2,1)} %bitcast.7, ...), custom_call_target="tpu_custom_call" | custom-call | tf_op jit(solution)/shard_map/block_backward/pallas_call | solution.py:449
  77.7 2.0 %finish.1 = (bf16[2,16,16,320]{3,2,1,0:T(8,128)(2,1)}, f32[5,320]{1,0:T(8,128)}, f32[180,320]{1,0:T(8,128)}) custom-call(bf16[16,16,640]{2,1,0:T(8,128)(2,1)} %get-tuple-element.9.gi_ref, bf16[16,16,128]{2,1,0:T(8,128)(2,1)} %get-tuple-element.10.attn_ref, bf16[16,32,128]{2,1,0:T(8,128)(2,1)} %get-tuple-element.11.conv_ref), custom_call_target="tpu_custom_call" | custom-call | tf_op jit(solution)/shard_map/finish/pallas_call | solution.py:498
